TPU v7x, 8 devices: a whole 2x2x1 slice. The times are simulated.
8 devices in a mesh: dp: 1 (over z), etp: 2 (over y), ep: 4 (over x, core).
Axes of the slice: x: 2, y: 2, z: 1, core: 2. Of those that a mesh axis runs over, the one named last changes fastest.
Arguments:
- hidden: bfloat16 [512, 2048], P(('dp', 'ep'))
- expert_ids: int32 [512, 2], P(('dp', 'ep'))
- gate_wts: float32 [512, 2], P(('dp', 'ep'))
- slot_pos: int32 [512, 2], P(('dp', 'ep'))
- w_gate: bfloat16 [8, 2048, 5632], P('ep', None, 'etp')
- w_up: bfloat16 [8, 2048, 5632], P('ep', None, 'etp')
- w_down: bfloat16 [8, 5632, 2048], P('ep', 'etp')
Outputs:
- output: bfloat16 [512, 2048], P(('dp', 'ep'))
All inputs are finite; a program needn't handle non-finite values.
Results may differ from a plain program's by a relative error of at most 0.0012.
Values are sent between devices in bfloat16 or wider.
A program may use at most 1 GiB of HBM per device.

v0:
```python
import jax
import jax.numpy as jnp
from jax import lax
from jax.sharding import PartitionSpec as P


def solution(mesh):
    group = mesh.shape['ep']
    row_spec = P(('dp', 'ep'), None)
    col_spec = P('ep', None, 'etp')
    in_specs = (row_spec, row_spec, row_spec, row_spec, col_spec, col_spec, P('ep', 'etp', None))

    def device_step(hidden, expert_ids, gate_wts, slot_pos, w_gate, w_up, w_down):
        rows_dev, d_model = hidden.shape
        top_k = expert_ids.shape[1]
        local_experts = w_gate.shape[0]
        experts = local_experts * group
        local_cap = ((5 * top_k * rows_dev) // (4 * experts) + 7) // 8 * 8
        capacity = group * local_cap
        tokens = rows_dev * group
        n_slots = local_experts * capacity
        all_hidden = lax.all_gather(hidden, 'ep', axis=0, tiled=True)
        all_ids = lax.all_gather(expert_ids, 'ep', axis=0, tiled=True)
        all_gates = lax.all_gather(gate_wts, 'ep', axis=0, tiled=True)
        all_pos = lax.all_gather(slot_pos, 'ep', axis=0, tiled=True)
        local_ids = all_ids - lax.axis_index('ep') * local_experts
        is_kept = (all_pos >= 0) & (local_ids >= 0) & (local_ids < local_experts)
        slot_index = jnp.where(is_kept, local_ids * capacity + all_pos, n_slots).reshape(-1)
        token_index = jnp.broadcast_to(jnp.arange(tokens, dtype=jnp.int32)[:, None], (tokens, top_k)).reshape(-1)
        slot_token = jnp.full((n_slots,), tokens, jnp.int32).at[slot_index].set(token_index, mode='drop')
        slot_gate = jnp.zeros((n_slots,), jnp.float32).at[slot_index].set(all_gates.reshape(-1), mode='drop')
        buffer = jnp.take(all_hidden, slot_token, axis=0, mode='fill', fill_value=0).reshape(local_experts, capacity, d_model)
        h_gate = jnp.einsum('ecd,edf->ecf', buffer, w_gate, preferred_element_type=jnp.float32)
        h_up = jnp.einsum('ecd,edf->ecf', buffer, w_up, preferred_element_type=jnp.float32)
        hidden_act = (jax.nn.silu(h_gate) * h_up).astype(jnp.bfloat16)
        expert_out = jnp.einsum('ecf,efd->ecd', hidden_act, w_down, preferred_element_type=jnp.float32)
        weighted = expert_out.reshape(n_slots, d_model) * slot_gate[:, None]
        part_sum = jax.ops.segment_sum(weighted, slot_token, num_segments=tokens)
        own_rows = lax.psum_scatter(part_sum, 'ep', scatter_dimension=0, tiled=True)
        summed = lax.psum(own_rows, 'etp')
        return summed.astype(jnp.bfloat16)

    return jax.shard_map(device_step, mesh=mesh, in_specs=in_specs, out_specs=row_spec, check_vma=False)
```

profile of v0, /device:TPU:1, one launch (start us, length us, event | category | flops | bytes accessed | tf_op | source)
XLA Modules:
  0.0 163.5 jit_solution(15302697572772848624)
XLA Ops:
  6.5 0.0 all-gather.2.cloned.1.call-start
  6.5 0.7 all-gather.2.cloned.1.call-update
  7.3 0.0 reduce-scatter.2.cloned.1.call-start
  7.3 7.2 %all_gather.13 = s32[512,2]{0,1:T(2,128)S(1)} all-gather(s32[128,2]{0,1:T(2,128)} %param.8), channel_id=1, replica_groups=mesh['dp'=1,'etp'=2,'ep'=4] {'ep'}, dimensions={0}, use_global_device_ids=true | all-gather | bytes 5120 | tf_op jit(solution)/shard_map/all_gather | solution.py:23
  14.5 7.9 %all_gather.12 = s32[512,2]{0,1:T(2,128)S(1)} all-gather(s32[128,2]{0,1:T(2,128)} %param.10), channel_id=1, replica_groups=mesh['dp'=1,'etp'=2,'ep'=4] {'ep'}, dimensions={0}, use_global_device_ids=true | all-gather | bytes 5120 | tf_op jit(solution)/shard_map/all_gather | solution.py:25
  22.4 0.1 copy.8
  22.5 0.2 reshape.53
  22.7 7.2 %all_gather.15 = f32[512,2]{0,1:T(2,128)S(1)} all-gather(f32[128,2]{0,1:T(2,128)} %param.9), channel_id=1, replica_groups=mesh['dp'=1,'etp'=2,'ep'=4] {'ep'}, dimensions={0}, use_global_device_ids=true | all-gather | bytes 5120 | tf_op jit(solution)/shard_map/all_gather | solution.py:24
  29.9 0.1 copy.9
  30.1 0.2 reshape.77
  30.3 0.2 reshape.69
  30.5 4.3 %scatter_custom_fusion = s32[320]{0:T(512)S(1)} fusion(s32[1024]{0:T(1024)S(1)} %bitcast.11, s32[1024]{0:T(1024)S(1)} %reshape.69, s32[]{:T(128)} %constant.11.clone.1), kind=kCustom, calls=%fused_computation.21 | custom fusion | bytes 1284 | tf_op jit(solution)/shard_map/scatter | solution.py:30
  34.8 0.1 broadcast_in_dim.44
  34.9 4.5 %scatter_custom_fusion.1 = f32[320]{0:T(512)S(1)} fusion(s32[1024]{0:T(1024)S(1)} %bitcast.12, f32[1024]{0:T(1024)S(1)} %reshape.77, f32[]{:T(128)} %constant.10.clone.1), kind=kCustom, calls=%fused_computation.19 | custom fusion | bytes 1284 | tf_op jit(solution)/shard_map/scatter | solution.py:31
  39.4 0.0 all-gather.2.cloned.1.call-done
  39.4 6.2 %gather_fusion = bf16[320,2048]{1,0:T(8,128)(2,1)S(1)} fusion(bf16[512,2048]{1,0:T(8,128)(2,1)} %all-gather.2.cloned.1.call-done, s32[1024]{0:T(1024)S(1)} %pad_clamp_fusion), kind=kCustom, calls=%fused_computation | custom fusion | bytes 2622720 | tf_op jit(solution)/shard_map/jit(_take)/gather | solution.py:32
  45.7 13.3 %fusion.3 = f32[2,160,2816]{2,1,0:T(8,128)} fusion(bf16[2,2048,2816]{2,1,0:T(8,128)(2,1)} %param.11, bf16[2,160,2048]{2,1,0:T(8,128)(2,1)S(1)} %bitcast.9, pred[2,160]{1,0:T(4,128)(4,1)S(1)} %broadcast_in_dim.44), kind=kOutput, calls=%fused_computation.10 | convolution fusion | flops 3691642880 | bytes 27984192 | tf_op jit(solution)/shard_map/ecd,edf->ecf/dot_general | solution.py:33
  59.0 20.8 %fusion.4 = f32[2,160,2048]{2,1,0:T(8,128)} fusion(bf16[2,2816,2048]{2,1,0:T(8,128)(2,1)} %param.13, bf16[2,2048,2816]{2,1,0:T(8,128)(2,1)} %param.12, f32[2,160,2816]{2,1,0:T(8,128)} %fusion.3, bf16[2,160,2048]{2,1,0:T(8,128)(2,1)S(1)} %bitcast.10, pred[2,160]{1,0:T(4,128)(4,1)S(1)} %broadcast_in_dim.44), kind=kOutput, calls=%fused_computation.11 | convolution fusion | flops 7388037120 | bytes 53674304 | tf_op jit(solution)/shard_map/ecf,efd->ecd/dot_general | solution.py:36
  79.8 2.0 %bitcast_multiply_fusion = f32[320,2048]{1,0:T(8,128)S(1)} fusion(f32[2,160,2048]{2,1,0:T(8,128)} %fusion.4, f32[320]{0:T(512)S(1)} %scatter_custom_fusion.1), kind=kLoop, calls=%fused_computation.6 | loop fusion | flops 655360 | bytes 5244160 | tf_op jit(solution)/shard_map/mul | solution.py:37
  81.8 6.8 %scatter_custom_fusion.2 = f32[512,2048]{1,0:T(8,128)} fusion(s32[320]{0:T(512)S(1)} %scatter_custom_fusion, f32[320,2048]{1,0:T(8,128)S(1)} %bitcast_multiply_fusion, f32[]{:T(128)} %constant.10.clone.1), kind=kCustom, calls=%fused_computation.7 | custom fusion | flops 655360 | bytes 4194308 | tf_op jit(solution)/shard_map/scatter-add | solution.py:38
  88.6 0.0 reduce-scatter.2.cloned.1.call-update
  88.6 39.9 %reduce-scatter.2.cloned.1.call-done = f32[128,2048]{1,0:T(8,128)} async-done(((f32[512,2048]{1,0:T(8,128)}), f32[128,2048]{1,0:T(8,128)}) %reduce-scatter.2.cloned.1.call-update) | async-done | bytes 1048592 | tf_op jit(solution)/shard_map/reduce_scatter | solution.py:39
  128.6 28.1 %all-reduce.1 = bf16[128,2048]{1,0:T(8,128)(2,1)} all-reduce(f32[128,2048]{1,0:T(8,128)} %reduce-scatter.2.cloned.1.call-done), channel_id=1, replica_groups=mesh['dp'=1,'etp'=2,'ep'=4] {'etp'}, use_global_device_ids=true, to_apply=%region_4.5 | all-reduce | flops 262144 | bytes 1572864 | tf_op jit(solution)/shard_map/psum | solution.py:40
  (6 shorter events, 0.1 us)
Async XLA Ops:
  6.5 32.9 %all-gather.2.cloned.1.call-start = ((), (), s32[]{:S(2)}) async-start(), calls=%async_computation.1 | async-start | bytes 2621440 | tf_op jit(solution)/shard_map/all_gather | solution.py:22
  7.3 121.3 %reduce-scatter.2.cloned.1.call-start = ((), (), s32[]{:S(2)}) async-start(), calls=%async_computation.2 | async-start | bytes 5242880 | tf_op jit(solution)/shard_map/reduce_scatter | solution.py:39
Sparse Core Ops, SparseCore 0:
  8.9 21.8 all-gather.1
  88.8 39.7 reduce-scatter.1
where the time goes:
time: 167 us; the launch traced here: 163 us
  blocking collectives  50.3 us (30%)
  waiting for transfers between devices  40.7 us (24%)
  matrix products  34.1 us (20%)
  local copies, waits for them, and re-layouts  15.9 us (10%)
  between operations  13.5 us (8%)
  other arithmetic  8.85 us (5%)
    reduce_scatter x1, waiting for transfers between devices, device_step(): own_rows = lax.psum_scatter(part_sum, 'ep', scatter_dimension=0, tiled=True)  39.9 us
    psum x1, blocking collectives, device_step(): summed = lax.psum(own_rows, 'etp')  28.1 us
    dot_general x1, matrix products, device_step(): jnp.einsum('ecf,efd->ecd', hidden_act, w_down, preferred_element_type=jnp...  20.8 us
    dot_general x1, matrix products, device_step(): jnp.einsum('ecd,edf->ecf', buffer, w_gate, preferred_element_type=jnp.flo...  13.3 us
    all_gather x1, blocking collectives, device_step(): all_pos = lax.all_gather(slot_pos, 'ep', axis=0, tiled=True)  7.89 us
    all_gather x1, blocking collectives, device_step(): all_gates = lax.all_gather(gate_wts, 'ep', axis=0, tiled=True)  7.2 us
    all_gather x1, blocking collectives, device_step(): all_ids = lax.all_gather(expert_ids, 'ep', axis=0, tiled=True)  7.19 us
    scatter-add x1, other arithmetic, device_step(): part_sum = jax.ops.segment_sum(weighted, slot_token, num_segments=tokens)  6.85 us
  transfers between devices with their start and end apart: 2, of which 1 were waited for; matrix products, arithmetic and copies ran while one was open for 6% of the time, Pallas kernels for 0%

commit v1 on v0

v1 whole, which is shorter than its diff:
```python
import functools
import jax
import jax.numpy as jnp
from jax import lax
from jax.sharding import PartitionSpec as P
from jax.experimental import pallas as pl
from jax.experimental.pallas import tpu as pltpu

MESH = pl.DeviceIdType.MESH
F32, BF16 = jnp.float32, jnp.bfloat16
N_Q = 4
N_U = 4
GU_SLOTS = 3
WD_SLOTS = 3
Y_FIRST = (0,)


def moe_kernel(rows, d_model, d_ff, cap_local,
               hid_hbm, ids_ref, gates_ref, pos_ref, wg_hbm, wu_hbm, wd_hbm, out_hbm,
               tok, route, onehot, comb, gate_col, xs, acc, act, wgu, wdn,
               w_own, w_send, w_recv, f1_keep, f1_send, f1_recv, f2_send, f2_recv, fin, outbuf,
               hid_sem, gu_sem, wd_sem, out_sem,
               rt_s, rt_r, s1_s, s1_r, xd_s, xd_r, yd_s, yd_r, c3_s, c3_r, c4_s, c4_r,
               dw_s, dw_r, f1_s, f1_r, f2_s, f2_r, fo_s, fo_r):
    cap = 4 * cap_local
    qw = d_model // N_Q
    hw = qw // 2
    uw = d_model // (2 * N_U)
    nh = d_ff // 2
    ep = lax.axis_index("ep")
    y = lax.axis_index("etp")
    c = lax.rem(ep, 2)
    x = ep // 2
    ox, oy, oc = 1 - x, 1 - y, 1 - c
    dev_c = {"ep": 2 * x + oc}
    dev_x = {"ep": 2 * ox + c}
    dev_xc = {"ep": 2 * ox + oc}
    dev_y = {"etp": oy}
    dev_yc = {"etp": oy, "ep": 2 * x + oc}
    dev_fin = {"etp": oy, "ep": 2 * x + y}

    def remote(src, dst, s, r, dev):
        return pltpu.make_async_remote_copy(src_ref=src, dst_ref=dst, send_sem=s, recv_sem=r,
                                            device_id=dev, device_id_type=MESH)

    hid_copy = pltpu.make_async_copy(hid_hbm, tok.at[pl.ds(ep * rows, rows)], hid_sem)
    hid_copy.start()

    def gu_copy(q, e, m):
        slot = (q % GU_SLOTS) * 2 + e
        src = (wg_hbm, wu_hbm)[m]
        return pltpu.make_async_copy(src.at[e, pl.ds(q * qw, qw)], wgu.at[slot, m], gu_sem.at[slot, m])

    def wd_copy(t, e):
        is_peer, u = unit_of(t)
        col = (jnp.where(is_peer, oc, c) * N_U + u) * uw
        slot = lax.rem(t, WD_SLOTS)
        return pltpu.make_async_copy(wd_hbm.at[e, :, pl.ds(pl.multiple_of(col, uw), uw)],
                                     wdn.at[slot, e], wd_sem.at[slot, e])

    def unit_of(t):
        is_peer = (t == 0) | ((lax.rem(t, 2) == 1) & (t < 2 * N_U - 1))
        return is_peer, jnp.where(is_peer, (t + 1) // 2, (t - 1) // 2)

    for q in range(GU_SLOTS):
        for e in range(2):
            for m in range(2):
                gu_copy(q, e, m).start()

    lane = lax.broadcasted_iota(jnp.int32, (rows, 128), 1)
    code = jnp.where(pos_ref[...] >= 0, ids_ref[...] * cap + pos_ref[...], -1).astype(F32)
    gts = gates_ref[...]
    cols = jnp.where(lane == 0, code[:, 0:1], jnp.where(lane == 1, code[:, 1:2],
                     jnp.where(lane == 2, gts[:, 0:1], gts[:, 1:2])))
    route[pl.ds(ep, 1)] = cols.T[0:8][None]

    barrier = pltpu.get_barrier_semaphore()
    for dev in (dev_c, dev_x, dev_xc, dev_y, dev_yc):
        pl.semaphore_signal(barrier, inc=1, device_id=dev, device_id_type=MESH)
    for t in range(WD_SLOTS):
        for e in range(2):
            wd_copy(jnp.int32(t), e).start()
    pl.semaphore_wait(barrier, 5)

    own = pl.ds(pl.multiple_of(ep * rows, rows), rows)
    of_c = pl.ds(pl.multiple_of((2 * x + oc) * rows, rows), rows)
    of_x = pl.ds(pl.multiple_of((2 * ox + c) * rows, rows), rows)
    of_xc = pl.ds(pl.multiple_of((2 * ox + oc) * rows, rows), rows)

    def piece(blk, q, half):
        start = q * qw if half is None else q * qw + half * hw
        return tok.at[blk, pl.ds(pl.multiple_of(start, 128), qw if half is None else hw)]

    def route_copy(i, dev, blk):
        return remote(route.at[blk], route.at[blk], rt_s.at[i], rt_r.at[i], dev)

    def s1(q, blk):
        return remote(piece(blk, q, None), piece(blk, q, None), s1_s.at[q], s1_r.at[q], dev_c)

    def s2(q, blk):
        return remote(piece(blk, q, y), piece(blk, q, y), xd_s.at[q], xd_r.at[q], dev_x)

    def s3y(q, half):
        return remote(piece(of_x, q, half), piece(of_x, q, half), yd_s.at[q], yd_r.at[q], dev_y)

    def s3c(q, blk):
        return remote(piece(blk, q, y), piece(blk, q, y), c3_s.at[q], c3_r.at[q], dev_c)

    def s4(q, blk):
        return remote(piece(blk, q, oy), piece(blk, q, oy), c4_s.at[q], c4_r.at[q], dev_c)

    for i, dev in enumerate((dev_c, dev_x, dev_xc)):
        route_copy(i, dev, ep).start()
    hid_copy.wait()
    for q in range(N_Q):
        s2(q, own).start()
    for q in range(N_Q):
        s1(q, own).start()

    @pl.loop(0, 4)
    def _(i):
        acc[i // 2, lax.rem(i, 2)] = jnp.zeros((cap, d_ff), F32)

    for i, blk in enumerate((2 * x + oc, 2 * ox + c, 2 * ox + oc)):
        route_copy(i, (dev_c, dev_x, dev_xc)[i], blk).wait_recv()

    def route_row(j):
        return jnp.concatenate([route[b, j:j + 1, :] for b in range(4)], axis=1)

    row_code = (route_row(0), route_row(1))
    row_gate = (route_row(2), route_row(3))
    for e in range(2):
        slot = (lax.broadcasted_iota(jnp.int32, (cap, 4 * rows), 0) + (2 * ep + e) * cap).astype(F32)
        hit0, hit1 = row_code[0] == slot, row_code[1] == slot
        onehot[e] = jnp.where(hit0 | hit1, 1.0, 0.0).astype(BF16)
        g = jnp.where(hit0, row_gate[0], 0.0) + jnp.where(hit1, row_gate[1], 0.0)
        gate_col[e] = jnp.sum(g, axis=1, keepdims=True)
    k = lax.broadcasted_iota(jnp.int32, (rows, 4 * cap_local), 1)
    part = jnp.where(k >= 2 * cap_local, 1, 0)
    k = k - part * (2 * cap_local)
    sub = jnp.where(k >= cap_local, 1, 0)
    k = k - sub * cap_local
    dev_of = jnp.where(part == 0, ep, 2 * x + oc)
    for b in range(4):
        slot = ((2 * dev_of + sub) * cap + b * cap_local + k).astype(F32)
        back = jnp.concatenate([route[b]] * 16, axis=0).T
        hit = (back[:, 0:1] == slot) | (back[:, 1:2] == slot)
        one = jnp.where(hit, 1.0, 0.0).astype(BF16)
        comb[b] = jnp.concatenate([one, one, one], axis=1)

    def relay_x(q):
        s2(q, of_x).wait_recv()
        s3y(q, y).start()
        s3c(q, of_x).start()

    def relay_y(q):
        s3y(q, oy).wait_recv()
        s4(q, of_x).start()

    relay_x(0)
    relay_x(1)
    relay_y(0)
    relay_x(2)
    between = {(0, 1): [(relay_y, 1)], (0, 2): [(relay_x, 3)], (0, 3): [(relay_y, 2)], (1, 1): [(relay_y, 3)]}

    for q in range(N_Q):
        s1(q, of_c).wait_recv()
        s3c(q, of_xc).wait_recv()
        s4(q, of_xc).wait_recv()
        for e in range(2):
            rows_q = jnp.dot(onehot[e], tok[:, q * qw:(q + 1) * qw], preferred_element_type=F32)
            xs[e] = rows_q.astype(BF16)

        @pl.loop(0, 4)
        def _(i, q=q):
            e, half = i // 2, lax.rem(i, 2)
            for j in (1, 2, 3):
                if (q, j) in between:
                    @pl.when(i == j)
                    def _(acts=between[(q, j)]):
                        for fn, arg in acts:
                            fn(arg)

            @pl.when(half == 0)
            def _():
                for m in range(2):
                    gu_copy(q, e, m).wait()

            span = pl.ds(pl.multiple_of(half * nh, 128), nh)
            slot = (q % GU_SLOTS) * 2 + e
            for m in range(2):
                acc[e, m, :, span] += jnp.dot(xs[e], wgu[slot, m, :, span], preferred_element_type=F32)
            if q + GU_SLOTS < N_Q:
                @pl.when(half == 1)
                def _():
                    for m in range(2):
                        gu_copy(q + GU_SLOTS, e, m).start()

    @pl.loop(0, 2 * 11)
    def _(i):
        e = i // 11
        span = pl.ds(pl.multiple_of(lax.rem(i, 11) * (d_ff // 11), 128), d_ff // 11)
        g = acc[e, 0, :, span]
        act[e, :, span] = (jax.nn.silu(g) * acc[e, 1, :, span]).astype(BF16)

    def dw(u):
        return remote(w_send.at[u], w_recv.at[u], dw_s.at[u], dw_r.at[u], dev_c)

    def first_dev(u):
        return dev_y if u in Y_FIRST else dev_x

    def second_dev(u):
        return dev_x if u in Y_FIRST else dev_y

    def f1(u):
        return remote(f1_send.at[u], f1_recv.at[u], f1_s.at[u], f1_r.at[u], first_dev(u))

    def f2(u):
        return remote(f2_send.at[u], f2_recv.at[u], f2_s.at[u], f2_r.at[u], second_dev(u))

    @pl.loop(0, 2 * N_U)
    def _(t):
        is_peer, u = unit_of(t)
        slot = lax.rem(t, WD_SLOTS)
        for e in range(2):
            wd_copy(t, e).wait()
        outs = [jnp.dot(act[e], wdn[slot, e], preferred_element_type=F32) * gate_col[e] for e in range(2)]

        @pl.when(is_peer)
        def _():
            for e in range(2):
                for b in range(4):
                    w_send[u, b, e * cap_local:(e + 1) * cap_local] = outs[e][b * cap_local:(b + 1) * cap_local]

        @pl.when(jnp.logical_not(is_peer))
        def _():
            for e in range(2):
                for b in range(4):
                    w_own[b, e * cap_local:(e + 1) * cap_local] = outs[e][b * cap_local:(b + 1) * cap_local]

        @pl.when(t + WD_SLOTS < 2 * N_U)
        def _():
            for e in range(2):
                wd_copy(t + WD_SLOTS, e).start()

        @pl.when(is_peer)
        def _():
            dw(u).start()

        @pl.when(jnp.logical_not(is_peer))
        def _():
            dw(u).wait_recv()
            y_first = functools.reduce(jnp.logical_or, [u == v for v in Y_FIRST], False)
            keep1 = jnp.where(y_first, 2 * ox + y, 2 * x + oy)
            send0 = jnp.where(y_first, 2 * x + oy, 2 * ox + y)
            for dst, pos, b in ((f1_send, 0, send0), (f1_send, 1, 2 * ox + oy),
                                (f1_keep, 0, 2 * x + y), (f1_keep, 1, keep1)):
                s = jnp.concatenate([w_own[b], w_recv[u, b]], axis=0)
                hi = s.astype(BF16)
                rest = s - hi.astype(F32)
                mid = rest.astype(BF16)
                lo = (rest - mid.astype(F32)).astype(BF16)
                parts = jnp.concatenate([hi, mid, lo], axis=0)
                dst[u, pos] = jnp.dot(comb[b], parts, preferred_element_type=F32)
            for v in range(N_U):
                @pl.when(u == v)
                def _(v=v):
                    f1(v).start()

    def out_cols(core, u):
        return pl.ds(pl.multiple_of((core * N_U + u) * uw, 128), uw)

    def to_other(u):
        return remote(fin.at[u], outbuf.at[:, out_cols(c, u)], fo_s.at[u, 0], fo_r.at[u, c], dev_fin)

    def to_core(u):
        return remote(fin.at[u], outbuf.at[:, out_cols(c, u)], fo_s.at[u, 1], fo_r.at[u, c], dev_c)

    def stage2(u):
        f1(u).wait_recv()
        f2_send[u] = f1_keep[u, 1] + f1_recv[u, 1]
        f2(u).start()
        f1_keep[u, 0] = f1_keep[u, 0] + f1_recv[u, 0]

    def stage3(u):
        f2(u).wait_recv()
        fin[u] = (f1_keep[u, 0] + f2_recv[u]).astype(BF16)
        to_other(u).start()

        @pl.when(c == y)
        def _():
            outbuf[:, out_cols(c, u)] = fin[u]

        @pl.when(c != y)
        def _():
            to_core(u).start()

    for u in range(N_U):
        stage2(u)
        if u >= 1:
            stage3(u - 1)
    stage3(N_U - 1)

    def incoming(u, core):
        return remote(fin.at[u], outbuf.at[:, out_cols(core, u)], fo_s.at[u, 0], fo_r.at[u, core], dev_fin)

    for u in range(N_U):
        incoming(u, oc).wait_recv()

        @pl.when(c != y)
        def _(u=u):
            incoming(u, c).wait_recv()

    out_copy = pltpu.make_async_copy(outbuf, out_hbm, out_sem)
    out_copy.start()

    for i, dev in enumerate((dev_c, dev_x, dev_xc)):
        route_copy(i, dev, ep).wait_send()
    for q in range(N_Q):
        s1(q, own).wait_send()
        s2(q, own).wait_send()
        s3y(q, y).wait_send()
        s3c(q, of_x).wait_send()
        s4(q, of_x).wait_send()
    for u in range(N_U):
        dw(u).wait_send()
        f1(u).wait_send()
        f2(u).wait_send()
        to_other(u).wait_send()

        @pl.when(c != y)
        def _(u=u):
            to_core(u).wait_send()
    out_copy.wait()


def solution(mesh):
    group = mesh.shape['ep']
    row_spec = P(('dp', 'ep'), None)
    col_spec = P('ep', None, 'etp')
    in_specs = (row_spec, row_spec, row_spec, row_spec, col_spec, col_spec, P('ep', 'etp', None))

    def device_step(hidden, expert_ids, gate_wts, slot_pos, w_gate, w_up, w_down):
        rows, d_model = hidden.shape
        top_k = expert_ids.shape[1]
        local_experts = w_gate.shape[0]
        experts = local_experts * group
        cap_local = ((5 * top_k * rows) // (4 * experts) + 7) // 8 * 8
        cap = group * cap_local
        d_ff = w_gate.shape[2]
        qw = d_model // N_Q
        uw = d_model // (2 * N_U)
        any_spec = pl.BlockSpec(memory_space=pl.ANY)
        vmem_spec = pl.BlockSpec(memory_space=pltpu.VMEM)
        dma = pltpu.SemaphoreType.DMA
        scratch = [
            pltpu.VMEM((group * rows, d_model), BF16),
            pltpu.VMEM((group, 8, 128), F32),
            pltpu.VMEM((2, cap, group * rows), BF16),
            pltpu.VMEM((group, rows, 12 * cap_local), BF16),
            pltpu.VMEM((2, cap, 1), F32),
            pltpu.VMEM((2, cap, qw), BF16),
            pltpu.VMEM((2, 2, cap, d_ff), F32),
            pltpu.VMEM((2, cap, d_ff), BF16),
            pltpu.VMEM((2 * GU_SLOTS, 2, qw, d_ff), BF16),
            pltpu.VMEM((WD_SLOTS, 2, d_ff, uw), BF16),
            pltpu.VMEM((4, 2 * cap_local, uw), F32),
            pltpu.VMEM((N_U, 4, 2 * cap_local, uw), F32),
            pltpu.VMEM((N_U, 4, 2 * cap_local, uw), F32),
            pltpu.VMEM((N_U, 2, rows, uw), F32),
            pltpu.VMEM((N_U, 2, rows, uw), F32),
            pltpu.VMEM((N_U, 2, rows, uw), F32),
            pltpu.VMEM((N_U, rows, uw), F32),
            pltpu.VMEM((N_U, rows, uw), F32),
            pltpu.VMEM((N_U, rows, uw), BF16),
            pltpu.VMEM((rows, d_model), BF16),
            dma, dma((2 * GU_SLOTS, 2)), dma((WD_SLOTS, 2)), dma,
            dma((3,)), dma((3,)),
        ] + [dma((N_Q,))] * 10 + [dma((N_U,))] * 6 + [dma((N_U, 2)), dma((N_U, 2))]
        return pl.pallas_call(
            functools.partial(moe_kernel, rows, d_model, d_ff, cap_local),
            out_shape=jax.ShapeDtypeStruct((rows, d_model), BF16),
            in_specs=[any_spec, vmem_spec, vmem_spec, vmem_spec, any_spec, any_spec, any_spec],
            out_specs=any_spec,
            scratch_shapes=scratch,
            compiler_params=pltpu.CompilerParams(collective_id=0, has_side_effects=True,
                                                 vmem_limit_bytes=67_043_328),
        )(hidden, expert_ids, gate_wts, slot_pos, w_gate, w_up, w_down)

    return jax.shard_map(device_step, mesh=mesh, in_specs=in_specs, out_specs=row_spec, check_vma=False)
```

time: 167 us -> 83.9 us (0.50); the launches traced: 163 us -> 83.6 us
  Pallas kernels: 0 us -> 77.5 us
  blocking collectives: 50.3 us -> 0 us
  waiting for transfers between devices: 40.7 us -> 0 us
  matrix products: 34.1 us -> 0 us
  between operations: 13.5 us -> 0.01 us
  local copies, waits for them, and re-layouts: 15.9 us -> 6.1 us
  other arithmetic: 8.85 us -> 0 us
    pallas_call x0 -> x1, Pallas kernels: none -> 77.5 us  [device_step(): pl.pallas_call(functools.partial(moe_kernel, rows, d_model, d_ff, cap_loc...]
    reduce_scatter x1 -> x0, waiting for transfers between devices: 39.9 us -> none  [device_step(): own_rows = lax.psum_scatter(part_sum, 'ep', scatter_dimension=0, tiled=True)]
    dot_general x2 -> x0, matrix products: 34.1 us -> none  [the longest x1 20.8 us: device_step(): jnp.einsum('ecf,efd->ecd', hidden_act, w_down, preferred_element_type=jnp...]
    psum x1 -> x0, blocking collectives: 28.1 us -> none  [device_step(): summed = lax.psum(own_rows, 'etp')]
    all_gather x3 -> x0, blocking collectives: 22.3 us -> none  [the longest x1 7.89 us: device_step(): all_pos = lax.all_gather(slot_pos, 'ep', axis=0, tiled=True)]
    scatter x2 -> x0, local copies, waits for them, and re-layouts: 8.78 us -> none  [the longest x1 4.48 us: device_step(): jnp.zeros((n_slots,), jnp.float32).at[slot_index]]
    scatter-add x1 -> x0, other arithmetic: 6.85 us -> none  [device_step(): part_sum = jax.ops.segment_sum(weighted, slot_token, num_segments=tokens)]
    gather x1 -> x0, local copies, waits for them, and re-layouts: 6.24 us -> none  [device_step(): jnp.take(all_hidden, slot_token, axis=0, mode='fill', fill_value=0)]
  transfers between devices with their start and end apart: 2 -> 0, of which waited for: 1 -> 0; matrix products, arithmetic and copies ran while one was open for 6% -> 0% of each run, Pallas kernels for 0% -> 0%
where the time goes in v1:
time: 83.9 us; the launch traced here: 83.6 us
  Pallas kernels  77.5 us (92%)
  local copies, waits for them, and re-layouts  6.1 us (7%)
    pallas_call x1, Pallas kernels, device_step(): pl.pallas_call(functools.partial(moe_kernel, rows, d_model, d_ff, cap_loc...  77.5 us
    unnamed x4, local copies, waits for them, and re-layouts  6.1 us

profile of v1, /device:TPU:1, one launch (start us, length us, event | category | flops | bytes accessed | tf_op | source)
XLA Modules:
  0.0 83.6 jit_solution(12942518202249936705)
XLA Ops:
  0.0 1.4 %copy.8.ids_ref = s32[128,2]{1,0:T(8,128)} copy(s32[128,2]{0,1:T(2,128)} %param.8) | data formatting | bytes 2048 | tf_op args[1]
  1.4 1.4 %copy.9.gates_ref = f32[128,2]{1,0:T(8,128)} copy(f32[128,2]{0,1:T(2,128)} %param.9) | data formatting | bytes 2048 | tf_op args[2]
  2.8 1.4 %copy.10.pos_ref = s32[128,2]{1,0:T(8,128)} copy(s32[128,2]{0,1:T(2,128)} %param.10) | data formatting | bytes 2048 | tf_op args[3]
  4.2 77.5 %shard_map.73 = bf16[128,2048]{1,0:T(8,128)(2,1)} custom-call(bf16[128,2048]{1,0:T(8,128)(2,1)} %hid_hbm.1, s32[128,2]{1,0:T(8,128)} %copy.8.ids_ref, f32[128,2]{1,0:T(8,128)} %copy.9.gates_ref, s32[128,2]{1,0:T(8,128)} %copy.10.pos_ref, bf16[2,2048,2816]{2,1,0:T(8,128)(2,1)} %wg_hbm.1, bf16[2,2048,2816]{2,1,0:T(8,128)(2,1)} %wu_hbm.1, ...), custom_call_target="tpu_custom_call" | custom-call | tf_op jit(solution)/shard_map/pallas_call | solution.py:380
  81.8 1.9 %copy.12 = bf16[128,2048]{1,0:T(8,128)(2,1)} copy(bf16[128,2048]{1,0:T(8,128)(2,1)} %shard_map.73) | data formatting | bytes 1048576

commit v2 on v0

v2 whole, which is shorter than its diff:
```python
import functools
import jax
import jax.numpy as jnp
from jax import lax
from jax.sharding import PartitionSpec as P
from jax.experimental import pallas as pl
from jax.experimental.pallas import tpu as pltpu

MESH = pl.DeviceIdType.MESH
F32, BF16 = jnp.float32, jnp.bfloat16
N_W = 4
GU_SLOTS = 3
WD_SLOTS = 3
N_U = 8
NB = 512
PIECE = 256
CHUNKS = ((0, 1, True), (1, 1, True), (2, 2, False), (4, 2, False), (6, 2, False))
Y_FIRST = (1, 3, 7)
ORDER = (
    "D0", "D1", "D2", "C0", "S0", "C1", "S1", "H0", "H1", "D3", "C2", "D4",
    "D5", "S2", "C3", "S3", "H2", "D6", "D7", "H3", "C5", "A0", "S5", "C4",
    "C6", "C7", "S7", "S6", "S4", "H5", "H7", "A2", "A3", "H6", "A1", "A6",
    "H4", "A5", "A4", "B2", "B6", "A7", "B0", "B5", "B1", "B4", "B3", "B7",
)


def moe_kernel(rows, d_model, d_ff, cap_local,
               hid_hbm, ids_ref, gates_ref, pos_ref, wg_hbm, wu_hbm, wd_hbm, out_hbm,
               tok, route, onehot, comb, gate_col, xs, acc, act, wgu, wdn,
               w_all, w_recv, f1_keep, f1_send, f1_recv, f2_send, f2_recv, fin,
               hid_sem, gu_sem, wd_sem,
               rt_s, rt_r, s1_s, s1_r, xd_s, xd_r, yd_s, yd_r, c3_s, c3_r, c4_s, c4_r,
               dw_s, dw_r, f1_s, f1_r, f2_s, f2_r, fo_s, fo_r):
    cap = 4 * cap_local
    kw = d_model // N_W
    uw = d_model // N_U
    hu = uw // 2
    ep = lax.axis_index("ep")
    y = lax.axis_index("etp")
    c = lax.rem(ep, 2)
    x = ep // 2
    ox, oy, oc = 1 - x, 1 - y, 1 - c
    dev_c = {"ep": 2 * x + oc}
    dev_x = {"ep": 2 * ox + c}
    dev_xc = {"ep": 2 * ox + oc}
    dev_y = {"etp": oy}
    dev_yc = {"etp": oy, "ep": 2 * x + oc}
    dev_fin = {"etp": oy, "ep": 2 * x + y}
    always = ep >= 0

    def remote(src, dst, s, r, dev):
        return pltpu.make_async_remote_copy(src_ref=src, dst_ref=dst, send_sem=s, recv_sem=r,
                                            device_id=dev, device_id_type=MESH)

    def block(b):
        return pl.ds(pl.multiple_of(b * rows, rows), rows)

    own, of_c, of_x, of_xc = block(ep), block(2 * x + oc), block(2 * ox + c), block(2 * ox + oc)

    def hid_copy(i):
        return pltpu.make_async_copy(hid_hbm.at[:, i * PIECE:(i + 1) * PIECE], tok.at[i, own], hid_sem.at[i])

    def gu_copy(w, e, m):
        slot = (w % GU_SLOTS) * 2 + e
        src = (wg_hbm, wu_hbm)[m]
        return pltpu.make_async_copy(src.at[e, pl.ds(w * kw, kw)], wgu.at[slot, m], gu_sem.at[slot, m])

    def wd_copy(u, e):
        slot = u % WD_SLOTS
        return pltpu.make_async_copy(wd_hbm.at[e, :, pl.ds(u * uw, uw)], wdn.at[slot, e], wd_sem.at[slot, e])

    for i in range(d_model // PIECE):
        hid_copy(i).start()

    code = jnp.where(pos_ref[...] >= 0, ids_ref[...] * cap + pos_ref[...], -1).astype(F32)
    route[ep] = jnp.concatenate([code, gates_ref[...], jnp.zeros((4, rows), F32)], axis=0)

    barrier = pltpu.get_barrier_semaphore()
    for dev in (dev_c, dev_x, dev_xc, dev_y, dev_yc):
        pl.semaphore_signal(barrier, inc=1, device_id=dev, device_id_type=MESH)
    with jax.named_scope("hid_wait"):
        for i in range(d_model // PIECE):
            hid_copy(i).wait()
    for w in range(GU_SLOTS):
        for e in range(2):
            for m in range(2):
                gu_copy(w, e, m).start(priority=1)
    for u in range(WD_SLOTS):
        for e in range(2):
            wd_copy(u, e).start(priority=1)
    with jax.named_scope("barrier"):
        pl.semaphore_wait(barrier, 5)

    def pieces(k, blk, half):
        first, n, direct = CHUNKS[k]
        return tok.at[pl.ds(first, n), blk] if half is None or direct else tok.at[first + half, blk]

    def route_copy(i, dev, b):
        return remote(route.at[b], route.at[b], rt_s.at[i], rt_r.at[i], dev)

    def to_core_own(k, blk):
        return remote(pieces(k, blk, None), pieces(k, blk, None), s1_s.at[k], s1_r.at[k], dev_c)

    def over_x(k, blk):
        return remote(pieces(k, blk, y), pieces(k, blk, y), xd_s.at[k], xd_r.at[k], dev_x)

    def over_y(k, half):
        return remote(pieces(k, of_x, half), pieces(k, of_x, half), yd_s.at[k], yd_r.at[k], dev_y)

    def to_core_x(k, blk):
        return remote(pieces(k, blk, y), pieces(k, blk, y), c3_s.at[k], c3_r.at[k], dev_c)

    def to_core_y(k, blk):
        return remote(pieces(k, blk, oy), pieces(k, blk, oy), c4_s.at[k], c4_r.at[k], dev_c)

    route_devs = (dev_c, dev_x, dev_xc)
    for i in range(3):
        route_copy(i, route_devs[i], ep).start()
    for k in range(len(CHUNKS)):
        over_x(k, own).start()
    for k in range(len(CHUNKS)):
        to_core_own(k, own).start()

    def relay_x(k):
        with jax.named_scope("relay_x"):
            over_x(k, of_x).wait_recv()
        if not CHUNKS[k][2]:
            over_y(k, y).start()
        to_core_x(k, of_x).start()

    def relay_y(k):
        with jax.named_scope("relay_y"):
            over_y(k, oy).wait_recv()
        to_core_y(k, of_x).start()

    with jax.named_scope("route_wait"):
        for i, b in enumerate((2 * x + oc, 2 * ox + c, 2 * ox + oc)):
            route_copy(i, route_devs[i], b).wait_recv()

    def route_row(j):
        return jnp.concatenate([route[b, j:j + 1, :] for b in range(4)], axis=1)

    row_code = (route_row(0), route_row(1))
    row_gate = (route_row(2), route_row(3))
    for e in range(2):
        slot = (lax.broadcasted_iota(jnp.int32, (cap, 4 * rows), 0) + (2 * ep + e) * cap).astype(F32)
        hit0, hit1 = row_code[0] == slot, row_code[1] == slot
        onehot[e] = jnp.where(hit0 | hit1, 1.0, 0.0).astype(BF16)
        g = jnp.where(hit0, row_gate[0], 0.0) + jnp.where(hit1, row_gate[1], 0.0)
        gate_col[e] = jnp.sum(g, axis=1, keepdims=True)

    def build_comb():
        k = lax.broadcasted_iota(jnp.int32, (rows, 4 * cap_local), 1)
        part = jnp.where(k >= 2 * cap_local, 1, 0)
        k = k - part * (2 * cap_local)
        sub = jnp.where(k >= cap_local, 1, 0)
        k = k - sub * cap_local
        dev_of = jnp.where(part == 0, ep, 2 * x + oc)
        with jax.named_scope("comb_mat"):
            for b in range(4):
                slot = ((2 * dev_of + sub) * cap + b * cap_local + k).astype(F32)
                back = jnp.concatenate([route[b]] * 16, axis=0).T
                hit = (back[:, 0:1] == slot) | (back[:, 1:2] == slot)
                one = jnp.where(hit, 1.0, 0.0).astype(BF16)
                comb[b] = jnp.concatenate([one, one, one], axis=1)

    relay_x(0)
    build_comb()
    relay_x(1)
    after = {(0, 1): [(relay_x, 2)],
             (1, 1): [(relay_x, 3), (relay_y, 2), (relay_x, 4)],
             (2, 0): [(relay_y, 3)], (2, 1): [(relay_y, 4)]}

    def product(k, e):
        first, n, _ = CHUNKS[k]
        w, off = first * PIECE // kw, first * PIECE % kw
        slot = (w % GU_SLOTS) * 2 + e
        width = n * PIECE
        last = k == len(CHUNKS) - 1
        for lo in range(0, d_ff, NB):
            span = slice(lo, min(lo + NB, d_ff))
            part = [jnp.dot(xs[e, :, 0:width], wgu[slot, m, off:off + width, span], preferred_element_type=F32)
                    for m in range(2)]
            if k > 0:
                part = [acc[e, m, :, span] + part[m] for m in range(2)]
            if last:
                act[e, :, span] = (jax.nn.silu(part[0]) * part[1]).astype(BF16)
            else:
                for m in range(2):
                    acc[e, m, :, span] = part[m]

    for k, (first, n, direct) in enumerate(CHUNKS):
        w, off = first * PIECE // kw, first * PIECE % kw
        with jax.named_scope("tok_wait"):
            to_core_own(k, of_c).wait_recv()
            to_core_x(k, of_xc).wait_recv()
            if not direct:
                to_core_y(k, of_xc).wait_recv()
        with jax.named_scope("gu_wait"):
            if off == 0:
                for e in range(2):
                    for m in range(2):
                        gu_copy(w, e, m).wait()
        groups = ((0,), (1,)) if (k, 0) in after else ((0, 1),)
        for gi, group in enumerate(groups):
            @pl.when(always)
            def _(k=k, first=first, n=n, group=group, gi=gi):
                with jax.named_scope("gu_dot"):
                    if gi == 0:
                        for e in range(2):
                            for i in range(n):
                                rows_k = jnp.dot(onehot[e], tok[first + i], preferred_element_type=F32)
                                xs[e, :, i * PIECE:(i + 1) * PIECE] = rows_k.astype(BF16)
                    for e in group:
                        product(k, e)
            for e in group:
                if off + n * PIECE == kw and w + GU_SLOTS < N_W:
                    for m in range(2):
                        gu_copy(w + GU_SLOTS, e, m).start(priority=1)
                for fn, arg in after.get((k, e), ()):
                    fn(arg)

    def dw(u):
        return remote(w_all.at[u, oc], w_recv.at[u], dw_s.at[u], dw_r.at[u], dev_c)

    def f1(u, pos):
        return remote(f1_send.at[u, pos], f1_recv.at[u, pos], f1_s.at[u, pos], f1_r.at[u, pos],
                      dev_y if u in Y_FIRST else dev_x)

    def f2(u):
        return remote(f2_send.at[u], f2_recv.at[u], f2_s.at[u], f2_r.at[u], dev_x if u in Y_FIRST else dev_y)

    def out_cols(core, u):
        return pl.ds(pl.multiple_of(u * uw + core * hu, hu), hu)

    def to_other(u):
        return remote(fin.at[u], out_hbm.at[:, out_cols(c, u)], fo_s.at[u, 0], fo_r.at[u, c], dev_fin)

    def to_core(u):
        return remote(fin.at[u], out_hbm.at[:, out_cols(c, u)], fo_s.at[u, 1], fo_r.at[u, c], dev_c)

    def to_self(u):
        return pltpu.make_async_copy(fin.at[u], out_hbm.at[:, out_cols(c, u)], fo_s.at[u, 1])

    def incoming(u, core):
        return remote(fin.at[u], out_hbm.at[:, out_cols(core, u)], fo_s.at[u, 0], fo_r.at[u, core], dev_fin)

    def down(u):
        slot = u % WD_SLOTS
        with jax.named_scope("wd_wait"):
            for e in range(2):
                wd_copy(u, e).wait()
        with jax.named_scope("wd_dot"):
            for e in range(2):
                out = jnp.dot(act[e], wdn[slot, e], preferred_element_type=F32) * gate_col[e]
                for core in range(2):
                    for b in range(4):
                        w_all[u, core, b, e * cap_local:(e + 1) * cap_local] = (
                            out[b * cap_local:(b + 1) * cap_local, core * hu:(core + 1) * hu])
        dw(u).start()
        if u + WD_SLOTS < N_U:
            for e in range(2):
                wd_copy(u + WD_SLOTS, e).start(priority=1)

    def combine(u):
        with jax.named_scope("dw_wait"):
            dw(u).wait_recv()
        if u in Y_FIRST:
            keep1, send0 = 2 * ox + y, 2 * x + oy
        else:
            keep1, send0 = 2 * x + oy, 2 * ox + y
        with jax.named_scope("comb"):
            for dst, pos, b in ((f1_send, 1, 2 * ox + oy), (f1_send, 0, send0),
                                (f1_keep, 1, keep1), (f1_keep, 0, 2 * x + y)):
                s = jnp.concatenate([w_all[u, c, b], w_recv[u, b]], axis=0)
                hi = s.astype(BF16)
                rest = s - hi.astype(F32)
                mid = rest.astype(BF16)
                lo = (rest - mid.astype(F32)).astype(BF16)
                parts = jnp.concatenate([hi, mid, lo], axis=0)
                dst[u, pos] = jnp.dot(comb[b], parts, preferred_element_type=F32)
    def second(u):
        with jax.named_scope("f1_wait"):
            f1(u, 1).wait_recv()
        f2_send[u] = f1_keep[u, 1] + f1_recv[u, 1]
        f2(u).start()

    def final(u):
        with jax.named_scope("f2_wait"):
            f1(u, 0).wait_recv()
            f2(u).wait_recv()
        fin[u] = (f1_keep[u, 0] + f1_recv[u, 0] + f2_recv[u]).astype(BF16)
        to_other(u).start()

        @pl.when(c == y)
        def _():
            to_self(u).start()

        @pl.when(c != y)
        def _():
            to_core(u).start()

    steps = {"D": down, "C": combine, "S": lambda u: f1(u, 1).start(), "H": lambda u: f1(u, 0).start(),
             "A": second, "B": final}
    for step in ORDER:
        steps[step[0]](int(step[1:]))

    with jax.named_scope("end"):
        for i in range(3):
            route_copy(i, route_devs[i], ep).wait_send()
        for k in range(len(CHUNKS)):
            to_core_own(k, own).wait_send()
            over_x(k, own).wait_send()
            to_core_x(k, of_x).wait_send()
            if not CHUNKS[k][2]:
                over_y(k, y).wait_send()
                to_core_y(k, of_x).wait_send()
        for u in range(N_U):
            dw(u).wait_send()
            f1(u, 0).wait_send()
            f1(u, 1).wait_send()
            f2(u).wait_send()
            to_other(u).wait_send()

            @pl.when(c != y)
            def _(u=u):
                to_core(u).wait_send()

            @pl.when(c == y)
            def _(u=u):
                to_self(u).wait()
    with jax.named_scope("in_wait"):
        for u in range(N_U):
            incoming(u, oc).wait_recv()

            @pl.when(c != y)
            def _(u=u):
                incoming(u, c).wait_recv()


def solution(mesh):
    group = mesh.shape['ep']
    row_spec = P(('dp', 'ep'), None)
    col_spec = P('ep', None, 'etp')
    in_specs = (row_spec, row_spec, row_spec, row_spec, col_spec, col_spec, P('ep', 'etp', None))

    def device_step(hidden, expert_ids, gate_wts, slot_pos, w_gate, w_up, w_down):
        rows, d_model = hidden.shape
        top_k = expert_ids.shape[1]
        local_experts = w_gate.shape[0]
        experts = local_experts * group
        cap_local = ((5 * top_k * rows) // (4 * experts) + 7) // 8 * 8
        cap = group * cap_local
        d_ff = w_gate.shape[2]
        hu = d_model // (2 * N_U)
        kw = d_model // N_W
        n_k = len(CHUNKS)
        any_spec = pl.BlockSpec(memory_space=pl.ANY)
        vmem_spec = pl.BlockSpec(memory_space=pltpu.VMEM)
        dma = pltpu.SemaphoreType.DMA
        scratch = [
            pltpu.VMEM((d_model // PIECE, group * rows, PIECE), BF16),
            pltpu.VMEM((group, 8, 128), F32),
            pltpu.VMEM((2, cap, group * rows), BF16),
            pltpu.VMEM((group, rows, 12 * cap_local), BF16),
            pltpu.VMEM((2, cap, 1), F32),
            pltpu.VMEM((2, cap, 2 * PIECE), BF16),
            pltpu.VMEM((2, 2, cap, d_ff), F32),
            pltpu.VMEM((2, cap, d_ff), BF16),
            pltpu.VMEM((2 * GU_SLOTS, 2, kw, d_ff), BF16),
            pltpu.VMEM((WD_SLOTS, 2, d_ff, 2 * hu), BF16),
            pltpu.VMEM((N_U, 2, 4, 2 * cap_local, hu), F32),
            pltpu.VMEM((N_U, 4, 2 * cap_local, hu), F32),
            pltpu.VMEM((N_U, 2, rows, hu), F32),
            pltpu.VMEM((N_U, 2, rows, hu), F32),
            pltpu.VMEM((N_U, 2, rows, hu), F32),
            pltpu.VMEM((N_U, rows, hu), F32),
            pltpu.VMEM((N_U, rows, hu), F32),
            pltpu.VMEM((N_U, rows, hu), BF16),
            dma((d_model // PIECE,)), dma((2 * GU_SLOTS, 2)), dma((WD_SLOTS, 2)),
            dma((3,)), dma((3,)),
        ] + [dma((n_k,))] * 10 + [dma((N_U,))] * 2 + [dma((N_U, 2))] * 2 + [dma((N_U,))] * 2 + [dma((N_U, 2))] * 2
        return pl.pallas_call(
            functools.partial(moe_kernel, rows, d_model, d_ff, cap_local),
            out_shape=jax.ShapeDtypeStruct((rows, d_model), BF16),
            in_specs=[any_spec, vmem_spec, vmem_spec, vmem_spec, any_spec, any_spec, any_spec],
            out_specs=any_spec,
            scratch_shapes=scratch,
            compiler_params=pltpu.CompilerParams(collective_id=0, has_side_effects=True,
                                                 vmem_limit_bytes=67_043_328),
        )(hidden, expert_ids.T, gate_wts.T, slot_pos.T, w_gate, w_up, w_down)

    return jax.shard_map(device_step, mesh=mesh, in_specs=in_specs, out_specs=row_spec, check_vma=False)
```

time: 167 us -> 52.2 us (0.31); the launches traced: 163 us -> 52 us
  blocking collectives: 50.3 us -> 0 us
  Pallas kernels: 0 us -> 50.1 us
  waiting for transfers between devices: 40.7 us -> 0 us
  matrix products: 34.1 us -> 0 us
  local copies, waits for them, and re-layouts: 15.9 us -> 1.88 us
  between operations: 13.5 us -> 0.01 us
  other arithmetic: 8.85 us -> 0 us
    pallas_call x0 -> x1, Pallas kernels: none -> 50.1 us  [device_step(): pl.pallas_call(functools.partial(moe_kernel, rows, d_model, d_ff, cap_loc...]
    reduce_scatter x1 -> x0, waiting for transfers between devices: 39.9 us -> none  [device_step(): own_rows = lax.psum_scatter(part_sum, 'ep', scatter_dimension=0, tiled=True)]
    dot_general x2 -> x0, matrix products: 34.1 us -> none  [the longest x1 20.8 us: device_step(): jnp.einsum('ecf,efd->ecd', hidden_act, w_down, preferred_element_type=jnp...]
    psum x1 -> x0, blocking collectives: 28.1 us -> none  [device_step(): summed = lax.psum(own_rows, 'etp')]
    all_gather x3 -> x0, blocking collectives: 22.3 us -> none  [the longest x1 7.89 us: device_step(): all_pos = lax.all_gather(slot_pos, 'ep', axis=0, tiled=True)]
    scatter x2 -> x0, local copies, waits for them, and re-layouts: 8.78 us -> none  [the longest x1 4.48 us: device_step(): jnp.zeros((n_slots,), jnp.float32).at[slot_index]]
    scatter-add x1 -> x0, other arithmetic: 6.85 us -> none  [device_step(): part_sum = jax.ops.segment_sum(weighted, slot_token, num_segments=tokens)]
    gather x1 -> x0, local copies, waits for them, and re-layouts: 6.24 us -> none  [device_step(): jnp.take(all_hidden, slot_token, axis=0, mode='fill', fill_value=0)]
  transfers between devices with their start and end apart: 2 -> 0, of which waited for: 1 -> 0; matrix products, arithmetic and copies ran while one was open for 6% -> 0% of each run, Pallas kernels for 0% -> 0%
where the time goes in v2:
time: 52.2 us; the launch traced here: 52 us
  Pallas kernels  50.1 us (96%)
  local copies, waits for them, and re-layouts  1.88 us (4%)
    pallas_call x1, Pallas kernels, device_step(): pl.pallas_call(functools.partial(moe_kernel, rows, d_model, d_ff, cap_loc...  50.1 us
    unnamed x1, local copies, waits for them, and re-layouts  1.88 us

profile of v2, /device:TPU:1, one launch (start us, length us, event | category | flops | bytes accessed | tf_op | source)
XLA Modules:
  0.0 52.0 jit_solution(8591400804164642229)
XLA Ops:
  0.0 50.1 %shard_map.73 = bf16[128,2048]{1,0:T(8,128)(2,1)} custom-call(bf16[128,2048]{1,0:T(8,128)(2,1)} %hid_hbm.1, s32[2,128]{1,0:T(2,128)} %bitcast.3, f32[2,128]{1,0:T(2,128)} %bitcast.4, s32[2,128]{1,0:T(2,128)} %bitcast.5, bf16[2,2048,2816]{2,1,0:T(8,128)(2,1)} %wg_hbm.1, bf16[2,2048,2816]{2,1,0:T(8,128)(2,1)} %wu_hbm.1, bf16[2,2816,2048]{2,1,0:T(8,128)(2,1)} %wd_hbm.1), custom_call_target="tpu_custom_call" | custom-call | tf_op jit(solution)/shard_map/pallas_call | solution.py:383
  50.1 1.9 %copy.9 = bf16[128,2048]{1,0:T(8,128)(2,1)} copy(bf16[128,2048]{1,0:T(8,128)(2,1)} %shard_map.73) | data formatting | bytes 1048576

commit v3 on v2

v3 whole, which is shorter than its diff:
```python
import functools
import jax
import jax.numpy as jnp
from jax import lax
from jax.sharding import PartitionSpec as P
from jax.experimental import pallas as pl
from jax.experimental.pallas import tpu as pltpu

MESH = pl.DeviceIdType.MESH
F32, BF16 = jnp.float32, jnp.bfloat16
N_W = 4
GU_SLOTS = 3
WD_SLOTS = 3
N_U = 8
NB = 512
PIECE = 256
Y_FIRST = (1, 3, 7)
ORDER = (
    "D0", "D1", "D2", "C0", "S0", "C1", "S1", "H0", "H1", "D3", "C2", "D4",
    "D5", "S2", "C3", "S3", "H2", "D6", "D7", "H3", "C5", "A0", "S5", "C4",
    "C6", "C7", "S7", "S6", "S4", "H5", "H7", "A2", "A3", "H6", "A1", "A6",
    "H4", "A5", "A4", "B2", "B6", "A7", "B0", "B5", "B1", "B4", "B3", "B7",
)


def moe_kernel(rows, d_model, d_ff, cap_local,
               hid_hbm, ids_hbm, gates_hbm, pos_hbm, wg_hbm, wu_hbm, wd_hbm, out_ref,
               ids, gates, pos, tok, route, onehot, comb, gate_col, xs, acc, act, wgu, wdn,
               w_all, w_recv, f1_keep, f1_send, f1_recv, f2_send, f2_recv, fin,
               in_sem, hid_sem, gu_sem, wd_sem, rt_s, rt_r, s1_s, s1_r, xd_s, xd_r, c3_s, c3_r,
               dw_s, dw_r, f1_s, f1_r, f2_s, f2_r, fo_s, fo_r):
    cap = 4 * cap_local
    kw = d_model // N_W
    uw = d_model // N_U
    hu = uw // 2
    n_k = d_model // PIECE
    ep = lax.axis_index("ep")
    y = lax.axis_index("etp")
    c = lax.rem(ep, 2)
    x = ep // 2
    ox, oy, oc = 1 - x, 1 - y, 1 - c
    dev_c = {"ep": 2 * x + oc}
    dev_x = {"ep": 2 * ox + c}
    dev_xc = {"ep": 2 * ox + oc}
    dev_y = {"etp": oy}
    dev_yc = {"etp": oy, "ep": 2 * x + oc}
    dev_fin = {"etp": oy, "ep": 2 * x + y}
    always = ep >= 0

    def remote(src, dst, s, r, dev):
        return pltpu.make_async_remote_copy(src_ref=src, dst_ref=dst, send_sem=s, recv_sem=r,
                                            device_id=dev, device_id_type=MESH)

    def block(b):
        return pl.ds(pl.multiple_of(b * rows, rows), rows)

    own, of_c, of_x, of_xc = block(ep), block(2 * x + oc), block(2 * ox + c), block(2 * ox + oc)

    barrier = pltpu.get_barrier_semaphore()
    for dev in (dev_c, dev_x, dev_xc, dev_y, dev_yc):
        pl.semaphore_signal(barrier, inc=1, device_id=dev, device_id_type=MESH)

    def hid_copy(i):
        return pltpu.make_async_copy(hid_hbm.at[:, i * PIECE:(i + 1) * PIECE], tok.at[i, own], hid_sem)

    hid_all = pltpu.make_async_copy(tok.at[:, own], tok.at[:, own], hid_sem)

    def gu_copy(w, e, m):
        slot = w % GU_SLOTS
        src = (wg_hbm, wu_hbm)[m]
        return pltpu.make_async_copy(src.at[e, pl.ds(w * kw, kw)], wgu.at[slot, e, m], gu_sem.at[slot])

    def gu_all(w):
        slot = w % GU_SLOTS
        return pltpu.make_async_copy(wgu.at[slot], wgu.at[slot], gu_sem.at[slot])

    def wd_copy(u):
        slot = u % WD_SLOTS
        return pltpu.make_async_copy(wd_hbm.at[:, :, pl.ds(u * uw, uw)], wdn.at[slot], wd_sem.at[slot])

    route_in = [pltpu.make_async_copy(src, dst, in_sem.at[i])
                for i, (src, dst) in enumerate(((ids_hbm, ids), (gates_hbm, gates), (pos_hbm, pos)))]
    for cp in route_in:
        cp.start()
    for i in range(n_k):
        hid_copy(i).start()

    for cp in route_in:
        cp.wait()
    code = jnp.where(pos[...] >= 0, ids[...] * cap + pos[...], -1).astype(F32)
    route[ep] = jnp.concatenate([code, gates[...], jnp.zeros((4, rows), F32)], axis=0)
    with jax.named_scope("hid_wait"):
        hid_all.wait()
    for w in range(GU_SLOTS):
        for e in range(2):
            for m in range(2):
                gu_copy(w, e, m).start(priority=1)
    with jax.named_scope("barrier"):
        pl.semaphore_wait(barrier, 5)

    def route_copy(i, b):
        return remote(route.at[b], route.at[b], rt_s, rt_r, route_devs[i])

    route_all = remote(route.at[pl.ds(0, 3)], route.at[pl.ds(0, 3)], rt_s, rt_r, dev_c)

    def to_core_own(k, blk):
        return remote(tok.at[k, blk], tok.at[k, blk], s1_s, s1_r, dev_c)

    def over_x(k, blk):
        return remote(tok.at[k, blk], tok.at[k, blk], xd_s, xd_r.at[k], dev_x)

    def to_core_x(k, blk):
        return remote(tok.at[k, blk], tok.at[k, blk], c3_s, c3_r.at[k], dev_c)

    route_devs = (dev_c, dev_x, dev_xc)
    for i in range(3):
        route_copy(i, ep).start()
    for k in range(n_k):
        over_x(k, own).start()
    for k in range(n_k):
        to_core_own(k, own).start()

    def relay_x(k):
        with jax.named_scope("relay_x"):
            over_x(k, of_x).wait_recv()
        to_core_x(k, of_x).start()

    with jax.named_scope("route_wait"):
        route_all.wait_recv()

    def route_row(j):
        return jnp.concatenate([route[b, j:j + 1, :] for b in range(4)], axis=1)

    row_code = (route_row(0), route_row(1))
    row_gate = (route_row(2), route_row(3))
    for e in range(2):
        slot = (lax.broadcasted_iota(jnp.int32, (cap, 4 * rows), 0) + (2 * ep + e) * cap).astype(F32)
        hit0, hit1 = row_code[0] == slot, row_code[1] == slot
        onehot[e] = jnp.where(hit0 | hit1, 1.0, 0.0).astype(BF16)
        g = jnp.where(hit0, row_gate[0], 0.0) + jnp.where(hit1, row_gate[1], 0.0)
        gate_col[e] = jnp.sum(g, axis=1, keepdims=True)

    def build_comb():
        k = lax.broadcasted_iota(jnp.int32, (rows, 4 * cap_local), 1)
        part = jnp.where(k >= 2 * cap_local, 1, 0)
        k = k - part * (2 * cap_local)
        sub = jnp.where(k >= cap_local, 1, 0)
        k = k - sub * cap_local
        dev_of = jnp.where(part == 0, ep, 2 * x + oc)
        with jax.named_scope("comb_mat"):
            for b in range(4):
                slot = ((2 * dev_of + sub) * cap + b * cap_local + k).astype(F32)
                back = jnp.concatenate([route[b]] * 16, axis=0).T
                hit = (back[:, 0:1] == slot) | (back[:, 1:2] == slot)
                one = jnp.where(hit, 1.0, 0.0).astype(BF16)
                comb[b] = jnp.concatenate([one, one, one], axis=1)

    def product(k, e):
        w, off = k * PIECE // kw, k * PIECE % kw
        slot = w % GU_SLOTS
        for lo in range(0, d_ff, NB):
            span = slice(lo, min(lo + NB, d_ff))
            part = [jnp.dot(xs[e], wgu[slot, e, m, off:off + PIECE, span], preferred_element_type=F32)
                    for m in range(2)]
            if k > 0:
                part = [acc[e, m, :, span] + part[m] for m in range(2)]
            if k == n_k - 1:
                act[e, :, span] = (jax.nn.silu(part[0]) * part[1]).astype(BF16)
            else:
                for m in range(2):
                    acc[e, m, :, span] = part[m]

    relay_x(0)
    build_comb()
    relay_x(1)
    with jax.named_scope("tok_wait"):
        remote(tok.at[:, of_c], tok.at[:, of_c], s1_s, s1_r, dev_c).wait_recv()
    for k in range(n_k):
        w, off = k * PIECE // kw, k * PIECE % kw
        with jax.named_scope("tok_wait"):
            to_core_x(k, of_xc).wait_recv()
        if off == 0:
            with jax.named_scope("gu_wait"):
                gu_all(w).wait()

        @pl.when(always)
        def _(k=k):
            with jax.named_scope("gu_dot"):
                for e in range(2):
                    xs[e] = jnp.dot(onehot[e], tok[k], preferred_element_type=F32).astype(BF16)
                for e in range(2):
                    product(k, e)

        if off + PIECE == kw and w + GU_SLOTS < N_W:
            for e in range(2):
                for m in range(2):
                    gu_copy(w + GU_SLOTS, e, m).start(priority=1)
        if k == n_k - 3:
            for u in range(WD_SLOTS):
                wd_copy(u).start(priority=1)
        if k + 2 < n_k:
            relay_x(k + 2)

    def dw(u):
        return remote(w_all.at[u, oc], w_recv.at[u], dw_s, dw_r.at[u], dev_c)

    def f1(u, pos):
        return remote(f1_send.at[u, pos], f1_recv.at[u, pos], f1_s, f1_r.at[u, pos],
                      dev_y if u in Y_FIRST else dev_x)

    def f2(u):
        return remote(f2_send.at[u], f2_recv.at[u], f2_s, f2_r.at[u], dev_x if u in Y_FIRST else dev_y)

    def out_cols(core, u):
        return pl.ds(pl.multiple_of(u * uw + core * hu, hu), hu)

    def to_other(u):
        return remote(fin.at[u], out_ref.at[:, out_cols(c, u)], fo_s.at[0], fo_r.at[c], dev_fin)

    def to_core(u):
        return remote(fin.at[u], out_ref.at[:, out_cols(c, u)], fo_s.at[1], fo_r.at[c], dev_c)

    def down(u):
        slot = u % WD_SLOTS
        with jax.named_scope("wd_wait"):
            wd_copy(u).wait()
        with jax.named_scope("wd_dot"):
            for e in range(2):
                out = jnp.dot(act[e], wdn[slot, e], preferred_element_type=F32) * gate_col[e]
                for core in range(2):
                    for b in range(4):
                        w_all[u, core, b, e * cap_local:(e + 1) * cap_local] = (
                            out[b * cap_local:(b + 1) * cap_local, core * hu:(core + 1) * hu])
        dw(u).start()
        if u + WD_SLOTS < N_U:
            wd_copy(u + WD_SLOTS).start(priority=1)

    def combine(u):
        with jax.named_scope("dw_wait"):
            dw(u).wait_recv()
        if u in Y_FIRST:
            keep1, send0 = 2 * ox + y, 2 * x + oy
        else:
            keep1, send0 = 2 * x + oy, 2 * ox + y
        with jax.named_scope("comb"):
            for dst, pos, b in ((f1_send, 1, 2 * ox + oy), (f1_send, 0, send0),
                                (f1_keep, 1, keep1), (f1_keep, 0, 2 * x + y)):
                s = jnp.concatenate([w_all[u, c, b], w_recv[u, b]], axis=0)
                hi = s.astype(BF16)
                rest = s - hi.astype(F32)
                mid = rest.astype(BF16)
                lo = (rest - mid.astype(F32)).astype(BF16)
                parts = jnp.concatenate([hi, mid, lo], axis=0)
                dst[u, pos] = jnp.dot(comb[b], parts, preferred_element_type=F32)
    def second(u):
        with jax.named_scope("f1_wait"):
            f1(u, 1).wait_recv()
        f2_send[u] = f1_keep[u, 1] + f1_recv[u, 1]
        f2(u).start()

    def final(u):
        with jax.named_scope("f2_wait"):
            f1(u, 0).wait_recv()
            f2(u).wait_recv()
        fin[u] = (f1_keep[u, 0] + f1_recv[u, 0] + f2_recv[u]).astype(BF16)
        to_other(u).start()

        @pl.when(c == y)
        def _():
            out_ref[:, out_cols(c, u)] = fin[u]

        @pl.when(c != y)
        def _():
            to_core(u).start()

    steps = {"D": down, "C": combine, "S": lambda u: f1(u, 1).start(), "H": lambda u: f1(u, 0).start(),
             "A": second, "B": final}
    for step in ORDER:
        steps[step[0]](int(step[1:]))

    with jax.named_scope("end"):
        route_all.wait_send()
        remote(tok.at[:, own], tok.at[:, own], s1_s, s1_r, dev_c).wait_send()
        remote(tok.at[:, own], tok.at[:, own], xd_s, xd_r.at[0], dev_x).wait_send()
        remote(tok.at[:, of_x], tok.at[:, of_x], c3_s, c3_r.at[0], dev_c).wait_send()
        remote(w_all.at[:, oc], w_recv, dw_s, dw_r.at[0], dev_c).wait_send()
        remote(f1_send, f1_recv, f1_s, f1_r.at[0, 0], dev_x).wait_send()
        remote(f2_send, f2_recv, f2_s, f2_r.at[0], dev_y).wait_send()
        remote(fin, fin, fo_s.at[0], fo_r.at[0], dev_fin).wait_send()

        @pl.when(c != y)
        def _():
            remote(fin, fin, fo_s.at[1], fo_r.at[0], dev_c).wait_send()
    with jax.named_scope("in_wait"):
        remote(fin, fin, fo_s.at[0], fo_r.at[oc], dev_fin).wait_recv()

        @pl.when(c != y)
        def _():
            remote(fin, fin, fo_s.at[0], fo_r.at[c], dev_fin).wait_recv()


def solution(mesh):
    group = mesh.shape['ep']
    row_spec = P(('dp', 'ep'), None)
    col_spec = P('ep', None, 'etp')
    in_specs = (row_spec, row_spec, row_spec, row_spec, col_spec, col_spec, P('ep', 'etp', None))

    def device_step(hidden, expert_ids, gate_wts, slot_pos, w_gate, w_up, w_down):
        rows, d_model = hidden.shape
        top_k = expert_ids.shape[1]
        local_experts = w_gate.shape[0]
        experts = local_experts * group
        cap_local = ((5 * top_k * rows) // (4 * experts) + 7) // 8 * 8
        cap = group * cap_local
        d_ff = w_gate.shape[2]
        hu = d_model // (2 * N_U)
        kw = d_model // N_W
        n_k = d_model // PIECE
        any_spec = pl.BlockSpec(memory_space=pl.ANY)
        vmem_spec = pl.BlockSpec(memory_space=pltpu.VMEM)
        dma = pltpu.SemaphoreType.DMA
        scratch = [
            pltpu.VMEM((top_k, rows), jnp.int32),
            pltpu.VMEM((top_k, rows), F32),
            pltpu.VMEM((top_k, rows), jnp.int32),
            pltpu.VMEM((d_model // PIECE, group * rows, PIECE), BF16),
            pltpu.VMEM((group, 8, 128), F32),
            pltpu.VMEM((2, cap, group * rows), BF16),
            pltpu.VMEM((group, rows, 12 * cap_local), BF16),
            pltpu.VMEM((2, cap, 1), F32),
            pltpu.VMEM((2, cap, PIECE), BF16),
            pltpu.VMEM((2, 2, cap, d_ff), F32),
            pltpu.VMEM((2, cap, d_ff), BF16),
            pltpu.VMEM((GU_SLOTS, 2, 2, kw, d_ff), BF16),
            pltpu.VMEM((WD_SLOTS, 2, d_ff, 2 * hu), BF16),
            pltpu.VMEM((N_U, 2, 4, 2 * cap_local, hu), F32),
            pltpu.VMEM((N_U, 4, 2 * cap_local, hu), F32),
            pltpu.VMEM((N_U, 2, rows, hu), F32),
            pltpu.VMEM((N_U, 2, rows, hu), F32),
            pltpu.VMEM((N_U, 2, rows, hu), F32),
            pltpu.VMEM((N_U, rows, hu), F32),
            pltpu.VMEM((N_U, rows, hu), F32),
            pltpu.VMEM((N_U, rows, hu), BF16),
            dma((3,)), dma, dma((GU_SLOTS,)), dma((WD_SLOTS,)), dma, dma, dma, dma,
            dma, dma((n_k,)), dma, dma((n_k,)),
            dma, dma((N_U,)), dma, dma((N_U, 2)), dma, dma((N_U,)), dma((2,)), dma((2,)),
        ]
        return pl.pallas_call(
            functools.partial(moe_kernel, rows, d_model, d_ff, cap_local),
            out_shape=pltpu.VMEM((rows, d_model), BF16),
            in_specs=[any_spec] * 7,
            out_specs=vmem_spec,
            scratch_shapes=scratch,
            compiler_params=pltpu.CompilerParams(collective_id=0, has_side_effects=True,
                                                 vmem_limit_bytes=66_400_000),
        )(hidden, expert_ids.T, gate_wts.T, slot_pos.T, w_gate, w_up, w_down)

    return jax.shard_map(device_step, mesh=mesh, in_specs=in_specs, out_specs=row_spec, check_vma=False)
```

time: 52.2 us -> 47.2 us (0.904)
  Pallas kernels: 50.1 us -> 46.2 us
  local copies, waits for them, and re-layouts: 1.88 us -> 0.8 us
    pallas_call x1, Pallas kernels: 50.1 us -> 46.2 us  [device_step(): pl.pallas_call(functools.partial(moe_kernel, rows, d_model, d_ff, cap_loc...]
    unnamed x1, local copies, waits for them, and re-layouts: 1.88 us -> 0.8 us
where the time goes in v3:
time: 47.2 us; the launch traced here: 47 us
  Pallas kernels  46.2 us (98%)
  local copies, waits for them, and re-layouts  0.8 us (2%)
    pallas_call x1, Pallas kernels, device_step(): pl.pallas_call(functools.partial(moe_kernel, rows, d_model, d_ff, cap_loc...  46.2 us

profile of v3, /device:TPU:1, one launch (start us, length us, event | category | flops | bytes accessed | tf_op | source)
XLA Modules:
  0.0 47.0 jit_solution(15506241337788098430)
XLA Ops:
  0.0 46.2 %shard_map.73 = bf16[128,2048]{1,0:T(8,128)(2,1)S(1)} custom-call(bf16[128,2048]{1,0:T(8,128)(2,1)} %hid_hbm.1, s32[2,128]{1,0:T(2,128)} %bitcast.3, f32[2,128]{1,0:T(2,128)} %bitcast.4, s32[2,128]{1,0:T(2,128)} %bitcast.5, bf16[2,2048,2816]{2,1,0:T(8,128)(2,1)} %wg_hbm.1, bf16[2,2048,2816]{2,1,0:T(8,128)(2,1)} %wu_hbm.1, bf16[2,2816,2048]{2,1,0:T(8,128)(2,1)} %wd_hbm.1), custom_call_target="tpu_custom_call" | custom-call | tf_op jit(solution)/shard_map/pallas_call | solution.py:348
  46.3 0.8 %copy.9 = bf16[128,2048]{1,0:T(8,128)(2,1)} copy(bf16[128,2048]{1,0:T(8,128)(2,1)S(1)} %shard_map.73) | data formatting | bytes 1048576

commit v4 on v3

--- a/solution.py
+++ b/solution.py
@@ -14,12 +14,13 @@
 N_U = 8
 NB = 512
 PIECE = 256
-Y_FIRST = (1, 3, 7)
+Y_FIRST = (0, 3, 5)
+AT_ONCE = (0, 1, 2, 3, 4)
 ORDER = (
-    "D0", "D1", "D2", "C0", "S0", "C1", "S1", "H0", "H1", "D3", "C2", "D4",
-    "D5", "S2", "C3", "S3", "H2", "D6", "D7", "H3", "C5", "A0", "S5", "C4",
-    "C6", "C7", "S7", "S6", "S4", "H5", "H7", "A2", "A3", "H6", "A1", "A6",
-    "H4", "A5", "A4", "B2", "B6", "A7", "B0", "B5", "B1", "B4", "B3", "B7",
+    "D0", "D1", "D2", "C0", "S0", "C1", "S1", "D3", "H0", "C2", "S2", "D4",
+    "C3", "S3", "H3", "H1", "D5", "H2", "D6", "C4", "S4", "D7", "A1", "C5",
+    "C6", "C7", "S6", "A2", "S5", "S7", "A3", "B1", "H7", "A6", "H6", "A5",
+    "H5", "A7", "A4", "B3", "H4", "B2", "A0", "B6", "B5", "B4", "B7", "B0",
 )
 
 
@@ -84,6 +85,10 @@
         cp.start()
     for i in range(n_k):
         hid_copy(i).start()
+    for w in range(GU_SLOTS):
+        for e in range(2):
+            for m in range(2):
+                gu_copy(w, e, m).start(priority=1)
 
     for cp in route_in:
         cp.wait()
@@ -91,10 +96,6 @@
     route[ep] = jnp.concatenate([code, gates[...], jnp.zeros((4, rows), F32)], axis=0)
     with jax.named_scope("hid_wait"):
         hid_all.wait()
-    for w in range(GU_SLOTS):
-        for e in range(2):
-            for m in range(2):
-                gu_copy(w, e, m).start(priority=1)
     with jax.named_scope("barrier"):
         pl.semaphore_wait(barrier, 5)
 
@@ -252,6 +253,8 @@
                 lo = (rest - mid.astype(F32)).astype(BF16)
                 parts = jnp.concatenate([hi, mid, lo], axis=0)
                 dst[u, pos] = jnp.dot(comb[b], parts, preferred_element_type=F32)
+                if dst is f1_send and pos == 1 and u in AT_ONCE:
+                    f1(u, 1).start()
     def second(u):
         with jax.named_scope("f1_wait"):
             f1(u, 1).wait_recv()
@@ -273,7 +276,7 @@
         def _():
             to_core(u).start()
 
-    steps = {"D": down, "C": combine, "S": lambda u: f1(u, 1).start(), "H": lambda u: f1(u, 0).start(),
+    steps = {"D": down, "C": combine, "S": lambda u: None if u in AT_ONCE else f1(u, 1).start(), "H": lambda u: f1(u, 0).start(),
              "A": second, "B": final}
     for step in ORDER:
         steps[step[0]](int(step[1:]))

time: 47.2 us -> 46.9 us (level)
  no operation moved by 1% of the time
where the time goes in v4:
time: 46.9 us
  Pallas kernels  46 us (98%)
  local copies, waits for them, and re-layouts  0.8 us (2%)
    pallas_call x1, Pallas kernels, device_step(): pl.pallas_call(functools.partial(moe_kernel, rows, d_model, d_ff, cap_loc...  46 us

profile of v4, /device:TPU:1, one launch (start us, length us, event | category | flops | bytes accessed | tf_op | source)
XLA Modules:
  0.0 46.9 jit_solution(1732313122034843135)
XLA Ops:
  0.0 46.0 %shard_map.73 = bf16[128,2048]{1,0:T(8,128)(2,1)S(1)} custom-call(bf16[128,2048]{1,0:T(8,128)(2,1)} %hid_hbm.1, s32[2,128]{1,0:T(2,128)} %bitcast.3, f32[2,128]{1,0:T(2,128)} %bitcast.4, s32[2,128]{1,0:T(2,128)} %bitcast.5, bf16[2,2048,2816]{2,1,0:T(8,128)(2,1)} %wg_hbm.1, bf16[2,2048,2816]{2,1,0:T(8,128)(2,1)} %wu_hbm.1, bf16[2,2816,2048]{2,1,0:T(8,128)(2,1)} %wd_hbm.1), custom_call_target="tpu_custom_call" | custom-call | tf_op jit(solution)/shard_map/pallas_call | solution.py:351
  46.1 0.8 %copy.9 = bf16[128,2048]{1,0:T(8,128)(2,1)} copy(bf16[128,2048]{1,0:T(8,128)(2,1)S(1)} %shard_map.73) | data formatting | bytes 1048576

commit v5 on v4

--- a/solution.py
+++ b/solution.py
@@ -12,15 +12,16 @@
 GU_SLOTS = 3
 WD_SLOTS = 3
 N_U = 8
-NB = 512
+NB = 256
 PIECE = 256
-Y_FIRST = (0, 3, 5)
-AT_ONCE = (0, 1, 2, 3, 4)
+PAIR = 2
+Y_FIRST = (1, 3, 5)
+AT_ONCE = (0, 1, 3, 7)
 ORDER = (
-    "D0", "D1", "D2", "C0", "S0", "C1", "S1", "D3", "H0", "C2", "S2", "D4",
-    "C3", "S3", "H3", "H1", "D5", "H2", "D6", "C4", "S4", "D7", "A1", "C5",
-    "C6", "C7", "S6", "A2", "S5", "S7", "A3", "B1", "H7", "A6", "H6", "A5",
-    "H5", "A7", "A4", "B3", "H4", "B2", "A0", "B6", "B5", "B4", "B7", "B0",
+    "D0", "D1", "D2", "C0", "S0", "C1", "S1", "H0", "D3", "C2", "H1", "D4",
+    "S2", "C3", "S3", "D5", "H3", "H2", "C4", "D6", "A0", "D7", "S4", "C5",
+    "A2", "A1", "S5", "H5", "C6", "C7", "S7", "A4", "A3", "S6", "H7", "A7",
+    "A5", "B2", "H4", "B1", "H6", "B0", "A6", "B3", "B7", "B5", "B4", "B6",
 )
 
 
@@ -28,7 +29,7 @@
                hid_hbm, ids_hbm, gates_hbm, pos_hbm, wg_hbm, wu_hbm, wd_hbm, out_ref,
                ids, gates, pos, tok, route, onehot, comb, gate_col, xs, acc, act, wgu, wdn,
                w_all, w_recv, f1_keep, f1_send, f1_recv, f2_send, f2_recv, fin,
-               in_sem, hid_sem, gu_sem, wd_sem, rt_s, rt_r, s1_s, s1_r, xd_s, xd_r, c3_s, c3_r,
+               in_sem, hid_sem, gu_sem, wd_sem, rt_s, rt_r, s1_s, s1_r, xd_s, xd_r, yd_s, yd_r, c3_s, c3_r,
                dw_s, dw_r, f1_s, f1_r, f2_s, f2_r, fo_s, fo_r):
     cap = 4 * cap_local
     kw = d_model // N_W
@@ -116,8 +117,22 @@
     route_devs = (dev_c, dev_x, dev_xc)
     for i in range(3):
         route_copy(i, ep).start()
+    mine, other = PAIR + y, PAIR + oy
+
+    def pair_over_x(blk):
+        return remote(tok.at[mine, blk], tok.at[mine, blk], xd_s, xd_r.at[PAIR], dev_x)
+
+    def pair_over_y(k):
+        return remote(tok.at[k, of_x], tok.at[k, of_x], yd_s, yd_r, dev_y)
+
+    def pair_to_core(k, i, blk):
+        return remote(tok.at[k, blk], tok.at[k, blk], c3_s, c3_r.at[PAIR + i], dev_c)
+
     for k in range(n_k):
-        over_x(k, own).start()
+        if k == PAIR:
+            pair_over_x(own).start()
+        elif k != PAIR + 1:
+            over_x(k, own).start()
     for k in range(n_k):
         to_core_own(k, own).start()
 
@@ -125,6 +140,17 @@
         with jax.named_scope("relay_x"):
             over_x(k, of_x).wait_recv()
         to_core_x(k, of_x).start()
+
+    def relay_pair():
+        with jax.named_scope("relay_p"):
+            pair_over_x(of_x).wait_recv()
+        pair_over_y(mine).start()
+        pair_to_core(mine, 0, of_x).start()
+
+    def relay_pair_y():
+        with jax.named_scope("relay_py"):
+            pair_over_y(other).wait_recv()
+        pair_to_core(other, 1, of_x).start()
 
     with jax.named_scope("route_wait"):
         route_all.wait_recv()
@@ -156,51 +182,73 @@
                 one = jnp.where(hit, 1.0, 0.0).astype(BF16)
                 comb[b] = jnp.concatenate([one, one, one], axis=1)
 
-    def product(k, e):
-        w, off = k * PIECE // kw, k * PIECE % kw
+    def product(e, w, off, width, first, last):
         slot = w % GU_SLOTS
+        depth = pl.ds(off, width)
         for lo in range(0, d_ff, NB):
             span = slice(lo, min(lo + NB, d_ff))
-            part = [jnp.dot(xs[e], wgu[slot, e, m, off:off + PIECE, span], preferred_element_type=F32)
+            part = [jnp.dot(xs[e, :, 0:width], wgu[slot, e, m, depth, span], preferred_element_type=F32)
                     for m in range(2)]
-            if k > 0:
+            if not first:
                 part = [acc[e, m, :, span] + part[m] for m in range(2)]
-            if k == n_k - 1:
+            if last:
                 act[e, :, span] = (jax.nn.silu(part[0]) * part[1]).astype(BF16)
             else:
                 for m in range(2):
                     acc[e, m, :, span] = part[m]
 
+    def gate_up(chunks, w, off, first=False, last=False):
+        @pl.when(always)
+        def _():
+            with jax.named_scope("gu_dot"):
+                for e in range(2):
+                    for i, k in enumerate(chunks):
+                        xs[e, :, i * PIECE:(i + 1) * PIECE] = jnp.dot(
+                            onehot[e], tok[k], preferred_element_type=F32).astype(BF16)
+                for e in range(2):
+                    product(e, w, off, len(chunks) * PIECE, first, last)
+
+    def have(*copies):
+        with jax.named_scope("tok_wait"):
+            for cp in copies:
+                cp.wait_recv()
+
+    def weights(w):
+        with jax.named_scope("gu_wait"):
+            gu_all(w).wait()
+
     relay_x(0)
     build_comb()
     relay_x(1)
-    with jax.named_scope("tok_wait"):
-        remote(tok.at[:, of_c], tok.at[:, of_c], s1_s, s1_r, dev_c).wait_recv()
-    for k in range(n_k):
-        w, off = k * PIECE // kw, k * PIECE % kw
-        with jax.named_scope("tok_wait"):
-            to_core_x(k, of_xc).wait_recv()
-        if off == 0:
-            with jax.named_scope("gu_wait"):
-                gu_all(w).wait()
-
-        @pl.when(always)
-        def _(k=k):
-            with jax.named_scope("gu_dot"):
-                for e in range(2):
-                    xs[e] = jnp.dot(onehot[e], tok[k], preferred_element_type=F32).astype(BF16)
-                for e in range(2):
-                    product(k, e)
-
-        if off + PIECE == kw and w + GU_SLOTS < N_W:
-            for e in range(2):
-                for m in range(2):
-                    gu_copy(w + GU_SLOTS, e, m).start(priority=1)
-        if k == n_k - 3:
-            for u in range(WD_SLOTS):
-                wd_copy(u).start(priority=1)
-        if k + 2 < n_k:
-            relay_x(k + 2)
+    have(remote(tok.at[:, of_c], tok.at[:, of_c], s1_s, s1_r, dev_c), to_core_x(0, of_xc))
+    weights(0)
+    gate_up((0,), 0, 0, first=True)
+    relay_pair()
+    have(to_core_x(1, of_xc))
+    gate_up((1,), 0, PIECE)
+    for e in range(2):
+        for m in range(2):
+            gu_copy(GU_SLOTS, e, m).start(priority=1)
+    relay_x(4)
+    have(pair_to_core(mine, 0, of_xc))
+    weights(1)
+    gate_up((mine,), 1, pl.multiple_of(y * PIECE, PIECE))
+    relay_x(5)
+    have(to_core_x(4, of_xc))
+    weights(2)
+    gate_up((4,), 2, 0)
+    relay_x(6)
+    relay_pair_y()
+    have(to_core_x(5, of_xc))
+    gate_up((5,), 2, PIECE)
+    relay_x(7)
+    have(pair_to_core(other, 1, of_xc))
+    gate_up((other,), 1, pl.multiple_of(oy * PIECE, PIECE))
+    for u in range(WD_SLOTS):
+        wd_copy(u).start(priority=1)
+    have(to_core_x(6, of_xc), to_core_x(7, of_xc))
+    weights(3)
+    gate_up((6, 7), 3, 0, last=True)
 
     def dw(u):
         return remote(w_all.at[u, oc], w_recv.at[u], dw_s, dw_r.at[u], dev_c)
@@ -284,7 +332,8 @@
     with jax.named_scope("end"):
         route_all.wait_send()
         remote(tok.at[:, own], tok.at[:, own], s1_s, s1_r, dev_c).wait_send()
-        remote(tok.at[:, own], tok.at[:, own], xd_s, xd_r.at[0], dev_x).wait_send()
+        remote(tok.at[pl.ds(0, n_k - 1), own], tok.at[pl.ds(0, n_k - 1), own], xd_s, xd_r.at[0], dev_x).wait_send()
+        pair_over_y(mine).wait_send()
         remote(tok.at[:, of_x], tok.at[:, of_x], c3_s, c3_r.at[0], dev_c).wait_send()
         remote(w_all.at[:, oc], w_recv, dw_s, dw_r.at[0], dev_c).wait_send()
         remote(f1_send, f1_recv, f1_s, f1_r.at[0, 0], dev_x).wait_send()
@@ -331,7 +380,7 @@
             pltpu.VMEM((2, cap, group * rows), BF16),
             pltpu.VMEM((group, rows, 12 * cap_local), BF16),
             pltpu.VMEM((2, cap, 1), F32),
-            pltpu.VMEM((2, cap, PIECE), BF16),
+            pltpu.VMEM((2, cap, 2 * PIECE), BF16),
             pltpu.VMEM((2, 2, cap, d_ff), F32),
             pltpu.VMEM((2, cap, d_ff), BF16),
             pltpu.VMEM((GU_SLOTS, 2, 2, kw, d_ff), BF16),
@@ -345,7 +394,7 @@
             pltpu.VMEM((N_U, rows, hu), F32),
             pltpu.VMEM((N_U, rows, hu), BF16),
             dma((3,)), dma, dma((GU_SLOTS,)), dma((WD_SLOTS,)), dma, dma, dma, dma,
-            dma, dma((n_k,)), dma, dma((n_k,)),
+            dma, dma((n_k,)), dma, dma, dma, dma((n_k,)),
             dma, dma((N_U,)), dma, dma((N_U, 2)), dma, dma((N_U,)), dma((2,)), dma((2,)),
         ]
         return pl.pallas_call(

time: 46.9 us -> 46.5 us (level)
  no operation moved by 1% of the time
where the time goes in v5:
time: 46.5 us; the launch traced here: 46.4 us
  Pallas kernels  45.6 us (98%)
  local copies, waits for them, and re-layouts  0.8 us (2%)
    pallas_call x1, Pallas kernels, device_step(): pl.pallas_call(functools.partial(moe_kernel, rows, d_model, d_ff, cap_loc...  45.6 us

profile of v5, /device:TPU:1, one launch (start us, length us, event | category | flops | bytes accessed | tf_op | source)
XLA Modules:
  0.0 46.4 jit_solution(11539071240369328586)
XLA Ops:
  0.0 45.6 %shard_map.73 = bf16[128,2048]{1,0:T(8,128)(2,1)S(1)} custom-call(bf16[128,2048]{1,0:T(8,128)(2,1)} %hid_hbm.1, s32[2,128]{1,0:T(2,128)} %bitcast.3, f32[2,128]{1,0:T(2,128)} %bitcast.4, s32[2,128]{1,0:T(2,128)} %bitcast.5, bf16[2,2048,2816]{2,1,0:T(8,128)(2,1)} %wg_hbm.1, bf16[2,2048,2816]{2,1,0:T(8,128)(2,1)} %wu_hbm.1, bf16[2,2816,2048]{2,1,0:T(8,128)(2,1)} %wd_hbm.1), custom_call_target="tpu_custom_call" | custom-call | tf_op jit(solution)/shard_map/pallas_call | solution.py:400
  45.6 0.8 %copy.9 = bf16[128,2048]{1,0:T(8,128)(2,1)} copy(bf16[128,2048]{1,0:T(8,128)(2,1)S(1)} %shard_map.73) | data formatting | bytes 1048576

commit v6 on v5

--- a/solution.py
+++ b/solution.py
@@ -15,13 +15,13 @@
 NB = 256
 PIECE = 256
 PAIR = 2
-Y_FIRST = (1, 3, 5)
-AT_ONCE = (0, 1, 3, 7)
+Y_FIRST = (1, 3, 7)
+AT_ONCE = (0, 1)
 ORDER = (
-    "D0", "D1", "D2", "C0", "S0", "C1", "S1", "H0", "D3", "C2", "H1", "D4",
-    "S2", "C3", "S3", "D5", "H3", "H2", "C4", "D6", "A0", "D7", "S4", "C5",
-    "A2", "A1", "S5", "H5", "C6", "C7", "S7", "A4", "A3", "S6", "H7", "A7",
-    "A5", "B2", "H4", "B1", "H6", "B0", "A6", "B3", "B7", "B5", "B4", "B6",
+    "D0", "D1", "D2", "C0", "S0", "C1", "S1", "D3", "H0", "C2", "H1", "D4",
+    "S2", "C3", "S3", "D5", "D6", "H2", "C4", "A0", "D7", "C6", "S4", "H3",
+    "S6", "C7", "A2", "A1", "S7", "A3", "H7", "C5", "S5", "B0", "A6", "A4",
+    "A7", "H6", "B2", "B1", "H4", "A5", "H5", "B3", "B6", "B4", "B7", "B5",
 )
 
 
@@ -29,7 +29,7 @@
                hid_hbm, ids_hbm, gates_hbm, pos_hbm, wg_hbm, wu_hbm, wd_hbm, out_ref,
                ids, gates, pos, tok, route, onehot, comb, gate_col, xs, acc, act, wgu, wdn,
                w_all, w_recv, f1_keep, f1_send, f1_recv, f2_send, f2_recv, fin,
-               in_sem, hid_sem, gu_sem, wd_sem, rt_s, rt_r, s1_s, s1_r, xd_s, xd_r, yd_s, yd_r, c3_s, c3_r,
+               in_sem, hid_sem, gu_sem, pair_sem, wd_sem, rt_s, rt_r, s1_s, s1_r, xd_s, xd_r, yd_s, yd_r, c3_s, c3_r,
                dw_s, dw_r, f1_s, f1_r, f2_s, f2_r, fo_s, fo_r):
     cap = 4 * cap_local
     kw = d_model // N_W
@@ -86,10 +86,25 @@
         cp.start()
     for i in range(n_k):
         hid_copy(i).start()
-    for w in range(GU_SLOTS):
+    pair_w = PAIR * PIECE // kw
+
+    def pair_rows(i):
+        return pl.ds(pl.multiple_of((y if i == 0 else oy) * PIECE, PIECE), PIECE)
+
+    def pair_copy(i, e, m):
+        src = (wg_hbm, wu_hbm)[m]
+        rows_in = pl.ds(pl.multiple_of(pair_w * kw + (y if i == 0 else oy) * PIECE, PIECE), PIECE)
+        return pltpu.make_async_copy(src.at[e, rows_in], wgu.at[pair_w, e, m, pair_rows(i)], pair_sem.at[i])
+
+    def pair_all(i):
+        half = wgu.at[pair_w, :, :, pair_rows(i)]
+        return pltpu.make_async_copy(half, half, pair_sem.at[i])
+
+    for load in ((lambda e, m: gu_copy(0, e, m)), (lambda e, m: pair_copy(0, e, m)),
+                 (lambda e, m: gu_copy(2, e, m)), (lambda e, m: pair_copy(1, e, m))):
         for e in range(2):
             for m in range(2):
-                gu_copy(w, e, m).start(priority=1)
+                load(e, m).start(priority=1)
 
     for cp in route_in:
         cp.wait()
@@ -231,7 +246,8 @@
             gu_copy(GU_SLOTS, e, m).start(priority=1)
     relay_x(4)
     have(pair_to_core(mine, 0, of_xc))
-    weights(1)
+    with jax.named_scope("gu_wait"):
+        pair_all(0).wait()
     gate_up((mine,), 1, pl.multiple_of(y * PIECE, PIECE))
     relay_x(5)
     have(to_core_x(4, of_xc))
@@ -243,6 +259,8 @@
     gate_up((5,), 2, PIECE)
     relay_x(7)
     have(pair_to_core(other, 1, of_xc))
+    with jax.named_scope("gu_wait"):
+        pair_all(1).wait()
     gate_up((other,), 1, pl.multiple_of(oy * PIECE, PIECE))
     for u in range(WD_SLOTS):
         wd_copy(u).start(priority=1)
@@ -393,7 +411,7 @@
             pltpu.VMEM((N_U, rows, hu), F32),
             pltpu.VMEM((N_U, rows, hu), F32),
             pltpu.VMEM((N_U, rows, hu), BF16),
-            dma((3,)), dma, dma((GU_SLOTS,)), dma((WD_SLOTS,)), dma, dma, dma, dma,
+            dma((3,)), dma, dma((GU_SLOTS,)), dma((2,)), dma((WD_SLOTS,)), dma, dma, dma, dma,
             dma, dma((n_k,)), dma, dma, dma, dma((n_k,)),
             dma, dma((N_U,)), dma, dma((N_U, 2)), dma, dma((N_U,)), dma((2,)), dma((2,)),
         ]

time: 46.5 us -> 46.5 us (level)
  no operation moved by 1% of the time
where the time goes in v6:
time: 46.5 us; the launch traced here: 46.4 us
  Pallas kernels  45.6 us (98%)
  local copies, waits for them, and re-layouts  0.8 us (2%)
    pallas_call x1, Pallas kernels, device_step(): pl.pallas_call(functools.partial(moe_kernel, rows, d_model, d_ff, cap_loc...  45.6 us

profile of v6, /device:TPU:1, one launch (start us, length us, event | category | flops | bytes accessed | tf_op | source)
XLA Modules:
  0.0 46.4 jit_solution(14019216882914811036)
XLA Ops:
  0.0 45.6 %shard_map.73 = bf16[128,2048]{1,0:T(8,128)(2,1)S(1)} custom-call(bf16[128,2048]{1,0:T(8,128)(2,1)} %hid_hbm.1, s32[2,128]{1,0:T(2,128)} %bitcast.3, f32[2,128]{1,0:T(2,128)} %bitcast.4, s32[2,128]{1,0:T(2,128)} %bitcast.5, bf16[2,2048,2816]{2,1,0:T(8,128)(2,1)} %wg_hbm.1, bf16[2,2048,2816]{2,1,0:T(8,128)(2,1)} %wu_hbm.1, bf16[2,2816,2048]{2,1,0:T(8,128)(2,1)} %wd_hbm.1), custom_call_target="tpu_custom_call" | custom-call | tf_op jit(solution)/shard_map/pallas_call | solution.py:418
  45.6 0.8 %copy.9 = bf16[128,2048]{1,0:T(8,128)(2,1)} copy(bf16[128,2048]{1,0:T(8,128)(2,1)S(1)} %shard_map.73) | data formatting | bytes 1048576

commit v7 on v6

--- a/solution.py
+++ b/solution.py
@@ -18,7 +18,7 @@
 Y_FIRST = (1, 3, 7)
 AT_ONCE = (0, 1)
 ORDER = (
-    "D0", "D1", "D2", "C0", "S0", "C1", "S1", "D3", "H0", "C2", "H1", "D4",
+    "D0", "D1", "D2", "C0", "C1", "R0", "H0", "R1", "D3", "C2", "H1", "D4",
     "S2", "C3", "S3", "D5", "D6", "H2", "C4", "A0", "D7", "C6", "S4", "H3",
     "S6", "C7", "A2", "A1", "S7", "A3", "H7", "C5", "S5", "B0", "A6", "A4",
     "A7", "H6", "B2", "B1", "H4", "A5", "H5", "B3", "B6", "B4", "B7", "B5",
@@ -305,13 +305,21 @@
     def combine(u):
         with jax.named_scope("dw_wait"):
             dw(u).wait_recv()
+        blocks(u, slice(0, 1 if u in AT_ONCE else 4))
+        if u in AT_ONCE:
+            f1(u, 1).start()
+
+    def rest(u):
+        blocks(u, slice(1, 4))
+
+    def blocks(u, which):
         if u in Y_FIRST:
             keep1, send0 = 2 * ox + y, 2 * x + oy
         else:
             keep1, send0 = 2 * x + oy, 2 * ox + y
         with jax.named_scope("comb"):
             for dst, pos, b in ((f1_send, 1, 2 * ox + oy), (f1_send, 0, send0),
-                                (f1_keep, 1, keep1), (f1_keep, 0, 2 * x + y)):
+                                (f1_keep, 1, keep1), (f1_keep, 0, 2 * x + y))[which]:
                 s = jnp.concatenate([w_all[u, c, b], w_recv[u, b]], axis=0)
                 hi = s.astype(BF16)
                 rest = s - hi.astype(F32)
@@ -319,8 +327,6 @@
                 lo = (rest - mid.astype(F32)).astype(BF16)
                 parts = jnp.concatenate([hi, mid, lo], axis=0)
                 dst[u, pos] = jnp.dot(comb[b], parts, preferred_element_type=F32)
-                if dst is f1_send and pos == 1 and u in AT_ONCE:
-                    f1(u, 1).start()
     def second(u):
         with jax.named_scope("f1_wait"):
             f1(u, 1).wait_recv()
@@ -342,7 +348,7 @@
         def _():
             to_core(u).start()
 
-    steps = {"D": down, "C": combine, "S": lambda u: None if u in AT_ONCE else f1(u, 1).start(), "H": lambda u: f1(u, 0).start(),
+    steps = {"D": down, "C": combine, "R": rest, "S": lambda u: f1(u, 1).start(), "H": lambda u: f1(u, 0).start(),
              "A": second, "B": final}
     for step in ORDER:
         steps[step[0]](int(step[1:]))

time: 46.5 us -> 46.6 us (level)
  no operation moved by 1% of the time
where the time goes in v7:
time: 46.6 us; the launch traced here: 46.5 us
  Pallas kernels  45.7 us (98%)
  local copies, waits for them, and re-layouts  0.8 us (2%)
    pallas_call x1, Pallas kernels, device_step(): pl.pallas_call(functools.partial(moe_kernel, rows, d_model, d_ff, cap_loc...  45.7 us

profile of v7, /device:TPU:1, one launch (start us, length us, event | category | flops | bytes accessed | tf_op | source)
XLA Modules:
  0.0 46.5 jit_solution(5694906023840249331)
XLA Ops:
  0.0 45.7 %shard_map.73 = bf16[128,2048]{1,0:T(8,128)(2,1)S(1)} custom-call(bf16[128,2048]{1,0:T(8,128)(2,1)} %hid_hbm.1, s32[2,128]{1,0:T(2,128)} %bitcast.3, f32[2,128]{1,0:T(2,128)} %bitcast.4, s32[2,128]{1,0:T(2,128)} %bitcast.5, bf16[2,2048,2816]{2,1,0:T(8,128)(2,1)} %wg_hbm.1, bf16[2,2048,2816]{2,1,0:T(8,128)(2,1)} %wu_hbm.1, bf16[2,2816,2048]{2,1,0:T(8,128)(2,1)} %wd_hbm.1), custom_call_target="tpu_custom_call" | custom-call | tf_op jit(solution)/shard_map/pallas_call | solution.py:424
  45.7 0.8 %copy.9 = bf16[128,2048]{1,0:T(8,128)(2,1)} copy(bf16[128,2048]{1,0:T(8,128)(2,1)S(1)} %shard_map.73) | data formatting | bytes 1048576
